TPU v7x, 32 devices: a whole 2x2x4 slice. The times are simulated.
32 devices in a mesh: tm: 4 (over y, core), lev: 8 (over z, x).
Axes of the slice: x: 2, y: 2, z: 4, core: 2. Of those that a mesh axis runs over, the one named last changes fastest.
Arguments:
- obs_cell: int32 [4, 16384], P('tm'), may hold values from 0 to 65535
- innovation: float32 [4, 64, 16384], P('tm', 'lev'), may hold values from -8 to 8
- tangent: float32 [4, 64, 128, 512], P('tm', 'lev'), may hold values from -0.45 to 0.45
- damping: float32 [4, 64, 128], P('tm'), may hold values from 0.05 to 0.95
- spread: float32 [64, 128], replicated, may hold values from 0.5 to 2
- vertical: float32 [64, 64], replicated, may hold values from -0.75 to 0.75
Outputs:
- gradient: float32 [64, 128, 2, 128], P(None, 'lev', None, 'tm')
All inputs are finite; a program needn't handle non-finite values.
Results may differ from a plain program's by a relative error of at most 0.0003.
Values sent between devices are 32-bit elements; how exact they have to be, the bound alone decides.
A program may use at most 128 MiB of HBM per device.

v0:
```python
import functools
import math

import jax
import jax.numpy as jnp
import numpy as np
from jax import lax
from jax.experimental import pallas as pl
from jax.experimental.pallas import tpu as pltpu
from jax.sharding import PartitionSpec as P

PRECISE = lax.Precision.HIGHEST
BF16 = jnp.bfloat16
F32 = jnp.float32
NT = (((1,), (1,)), ((), ()))
NN = (((1,), (0,)), ((), ()))
VMEM_BYTES = 62 * 1024 * 1024


def dot(left, right, dims):
    return lax.dot_general(left, right, dims, preferred_element_type=F32)


def halves(value):
    high = value.astype(BF16)
    return high, (value - high.astype(F32)).astype(BF16)


def fourier_rows(lon_count, wave_count):
    index = np.arange(wave_count)[:, None] * np.arange(lon_count)[None, :] % lon_count
    angles = 2.0 * np.pi * index / lon_count
    return (np.concatenate([np.cos(angles), np.sin(angles)], 0) * np.sqrt(2.0 / lon_count)).astype(np.float32)


def legendre_coefficients(lat_count, wave_count):
    phi = (np.arange(lat_count) + 0.5) * np.pi / lat_count - 0.5 * np.pi
    orders = np.arange(wave_count).astype(np.float64)
    lead = np.array(
        [
            -0.5 * math.log(2.0)
            + 0.5 * (math.lgamma(m + 1.5) - math.lgamma(1.5) - math.lgamma(m + 1.0))
            for m in range(wave_count)
        ]
    )
    weight = np.sqrt(np.pi * np.cos(phi) / lat_count)
    diagonal = weight[:, None] * np.exp(lead[None, :] + orders[None, :] * np.log(np.cos(phi))[:, None])
    mu = np.broadcast_to(np.sin(phi)[:, None], (lat_count, wave_count))
    degree = orders[:, None]
    above = degree > orders[None, :]
    gap = np.where(above, degree**2 - orders[None, :] ** 2, 1.0)
    up = np.where(above, np.sqrt(np.maximum(4.0 * degree**2 - 1.0, 0.0) / gap), 0.0)
    lower = degree - 1.0
    down = np.sqrt(np.maximum(lower**2 - orders[None, :] ** 2, 0.0) / np.maximum(4.0 * lower**2 - 1.0, 1.0))
    both = up * down
    return [np.asarray(a, np.float32) for a in (mu, diagonal, up, both)]


def forcing_kernel(lat_rows, lon_cols, cell_ref, innov_ref, out_ref):
    cells = cell_ref[0]
    width = cells.shape[1]
    rows = cells // lon_cols
    cols = cells - rows * lon_cols
    innov = innov_ref[0]
    levels = innov.shape[0]
    hit = lax.broadcasted_iota(jnp.int32, (lat_rows, width), 0) == rows
    spread_cols = jnp.where(
        lax.broadcasted_iota(jnp.int32, (lon_cols, width), 0) == cols, 1.0, 0.0
    ).astype(BF16)
    high = innov.astype(BF16).astype(F32)
    low = innov - high
    pieces = [jnp.where(hit, part[k : k + 1, :], 0.0).astype(BF16) for part in (high, low) for k in range(levels)]
    field = dot(jnp.concatenate(pieces, 0), spread_cols, NT)
    field = field[: levels * lat_rows] + field[levels * lat_rows :]

    @pl.when(pl.program_id(1) == 0)
    def _():
        out_ref[0] = field

    @pl.when(pl.program_id(1) > 0)
    def _():
        out_ref[0] += field


def forcing_fields(cells, innov, lat_rows, lon_cols):
    times, levels, count = innov.shape
    width = math.gcd(count, 2048)
    body = functools.partial(forcing_kernel, lat_rows, lon_cols)
    return pl.pallas_call(
        body,
        grid=(times, count // width),
        in_specs=[
            pl.BlockSpec((1, 1, width), lambda t, c: (t, 0, c)),
            pl.BlockSpec((1, levels, width), lambda t, c: (t, 0, c)),
        ],
        out_specs=pl.BlockSpec((1, levels * lat_rows, lon_cols), lambda t, c: (t, 0, 0)),
        out_shape=jax.ShapeDtypeStruct((times, levels * lat_rows, lon_cols), F32),
        compiler_params=pltpu.CompilerParams(vmem_limit_bytes=VMEM_BYTES),
        cost_estimate=pl.CostEstimate(
            flops=4 * times * levels * lat_rows * lon_cols * count, bytes_accessed=8 * 2**20, transcendentals=0
        ),
    )(cells.reshape(times, 1, count), innov)


def sweep_kernel(
    field_ref, tangent_ref, damp_ref, fhigh_ref, flow_ref, mu_ref, diag_ref, up_ref, both_ref,
    total_ref, table, high, low, packed, adjoint,
):
    times, rows, lon_cols = field_ref.shape
    lat_rows, waves = mu_ref.shape
    levels = rows // lat_rows
    group = damp_ref.shape[1]
    half = group // 2

    orders = lax.broadcasted_iota(jnp.int32, (lat_rows, waves), 1)

    def advance(n, state):
        one, two = state
        recurred = up_ref[pl.ds(n, 1), :] * (mu_ref[...] * one) - both_ref[pl.ds(n, 1), :] * two
        value = jnp.where(orders == n, diag_ref[...], recurred)
        table[pl.ds(n, waves, stride=waves), :] = value.T
        return value, one

    zero = 0.0 * mu_ref[...]
    lax.fori_loop(0, waves, advance, (zero, zero), unroll=8)

    def split(m, carry):
        upper, lower = halves(table[pl.ds(m * waves, waves), :])
        high[m] = upper
        low[m] = lower
        return carry

    lax.fori_loop(0, waves, split, 0, unroll=4)

    def pair_sum(value):
        return value + pltpu.roll(value, half, 0)

    in_high = lax.broadcasted_iota(jnp.int32, (group, waves), 0) < half
    adjoint[...] = jnp.zeros_like(adjoint)
    total_ref[...] = jnp.zeros_like(total_ref)

    def analyse(t):
        forced = adjoint[...] + field_ref[t]
        adjoint[...] = forced
        for k in range(levels):
            upper, lower = halves(forced[k * lat_rows : (k + 1) * lat_rows])
            coeffs = (
                dot(fhigh_ref[...], upper, NT) + dot(flow_ref[...], upper, NT) + dot(fhigh_ref[...], lower, NT)
            )
            for p in range(2):
                part = coeffs[p * waves : (p + 1) * waves]
                rounded = part.astype(BF16).astype(F32)
                packed[pl.ds(2 * k + p, waves, stride=group), :] = rounded
                packed[pl.ds(half + 2 * k + p, waves, stride=group), :] = part - rounded

    batch = math.gcd(waves, 16)

    def lanes_of(b):
        return pl.ds(pl.multiple_of(b * batch * group, batch * group), batch * group)

    def parts_of(value):
        return [value[u * group : (u + 1) * group] for u in range(batch)]

    def product(lefts, b, dims):
        return [
            pair_sum(dot(left, high[b * batch + u], dims) + dot(left, low[b * batch + u], dims))
            for u, left in enumerate(lefts)
        ]

    def spectral_of(b):
        lefts = parts_of(packed[lanes_of(b), :].astype(BF16))
        values = product(lefts, b, NT)
        total_ref[lanes_of(b), :] += jnp.concatenate(values, 0)
        return values

    def step(s, carry):
        t = times - 1 - s
        analyse(t)
        damp = damp_ref[t]

        def wave(b, inner):
            lefts = []
            for value in spectral_of(b):
                filtered = value * damp
                rounded = filtered.astype(BF16).astype(F32)
                lefts.append(jnp.where(in_high, rounded, filtered - rounded).astype(BF16))
            packed[lanes_of(b), :] = jnp.concatenate(product(lefts, b, NN), 0)
            return inner

        lax.fori_loop(0, waves // batch, wave, 0)
        for k in range(levels):
            synth = jnp.concatenate(
                [packed[pl.ds(2 * k + p, waves, stride=group), :] for p in range(2)], 0
            ).T
            upper, lower = halves(synth)
            gridded = dot(upper, fhigh_ref[...], NN) + dot(lower, fhigh_ref[...], NN) + dot(upper, flow_ref[...], NN)
            place = pl.ds(k * lat_rows, lat_rows)
            adjoint[place, :] = tangent_ref[t, place, :] * adjoint[place, :] + gridded
        return carry

    lax.fori_loop(0, times - 1, step, 0)
    analyse(0)

    def last(b, inner):
        spectral_of(b)
        return inner

    lax.fori_loop(0, waves // batch, last, 0)


def sweep(fields, tangent, damp, lat_rows, waves):
    times, rows, lon_cols = fields.shape
    group = damp.shape[1]
    fourier = fourier_rows(lon_cols, waves)
    fhigh = fourier.astype(jnp.bfloat16)
    flow = (fourier - fhigh.astype(np.float32)).astype(jnp.bfloat16)
    mu, diagonal, up, both = legendre_coefficients(lat_rows, waves)
    return pl.pallas_call(
        sweep_kernel,
        in_specs=[pl.BlockSpec(memory_space=pltpu.VMEM)] * 9,
        out_specs=pl.BlockSpec(memory_space=pltpu.VMEM),
        out_shape=jax.ShapeDtypeStruct((waves * group, waves), F32),
        scratch_shapes=[
            pltpu.VMEM((waves * waves, lat_rows), F32),
            pltpu.VMEM((waves, waves, lat_rows), BF16),
            pltpu.VMEM((waves, waves, lat_rows), BF16),
            pltpu.VMEM((waves * group, lat_rows), F32),
            pltpu.VMEM((rows, lon_cols), F32),
        ],
        compiler_params=pltpu.CompilerParams(vmem_limit_bytes=VMEM_BYTES),
    )(fields, tangent, damp, fhigh, flow, mu, diagonal, up, both)


def shards(obs_cell, innovation, tangent, damping, spread, vertical):
    sections = lax.axis_size("tm")
    groups = lax.axis_size("lev")
    me_tm = lax.axis_index("tm")
    me_lev = lax.axis_index("lev")
    lev_dev, lat_rows, lon_cols = tangent.shape[1:]
    levels, waves = damping.shape[1:]
    mine = -(-lev_dev // sections)
    mine += mine % 2
    padded = mine * sections

    def pad_levels(value, axis):
        widths = [(0, 0)] * value.ndim
        widths[axis] = (0, padded - value.shape[axis])
        return jnp.pad(value, widths) if padded > value.shape[axis] else value

    count = obs_cell.shape[1]
    damp_block = pad_levels(lax.dynamic_slice_in_dim(damping[0], me_lev * lev_dev, lev_dev, 0), 0)
    damp_block = damp_block.reshape(sections, mine * waves)
    damp_deep = -(-mine * waves // count)
    damp_block = jnp.pad(damp_block, ((0, 0), (0, damp_deep * count - mine * waves)))
    message = jnp.concatenate(
        [
            pad_levels(innovation[0], 0).reshape(sections, mine, count),
            jnp.broadcast_to(obs_cell.astype(F32)[None], (sections, 1, count)),
            damp_block.reshape(sections, damp_deep, count),
        ],
        1,
    )
    message = lax.all_to_all(message, "tm", split_axis=0, concat_axis=0, tiled=True)
    innov = message[:, :mine]
    cells = message[:, mine].astype(jnp.int32)
    damp_mine = message[:, mine + 1 :].reshape(sections, damp_deep * count)[:, : mine * waves]
    damp_mine = damp_mine.reshape(sections, mine, waves)
    rates = lax.all_to_all(
        pad_levels(tangent[0], 0).reshape(sections, mine * lat_rows, lon_cols),
        "tm", split_axis=0, concat_axis=0, tiled=True,
    )
    fields = forcing_fields(cells, innov, lat_rows, lon_cols)
    damp_rows = jnp.tile(jnp.repeat(damp_mine, 2, axis=1), (1, 2, 1))
    total = sweep(fields, rates, damp_rows, lat_rows, waves)

    block_m = waves // groups
    block_n = waves // sections
    outgoing = total.reshape(waves, 4 * mine, waves)[:, : 2 * mine].reshape(groups, block_m, mine, 2, sections, block_n)
    outgoing = outgoing.transpose(0, 4, 2, 1, 3, 5).reshape(groups * sections, mine, block_m * 2 * block_n)
    arrived = lax.all_to_all(outgoing, ("lev", "tm"), split_axis=0, concat_axis=0, tiled=True)
    arrived = arrived.reshape(groups, padded, block_m * 2, block_n)[:, :lev_dev]
    arrived = arrived.reshape(levels, block_m * 2, block_n)
    spread_cols = lax.dynamic_slice_in_dim(spread, me_tm * block_n, block_n, 1)
    scaled = (arrived * spread_cols[:, None, :]).reshape(levels, block_m * 2 * block_n)
    result = jnp.einsum("kj,kx->jx", vertical, scaled, precision=PRECISE)
    return result.reshape(levels, block_m, 2, block_n)


def solution(mesh):
    placed = (
        P("tm", None),
        P("tm", "lev", None),
        P("tm", "lev", None, None),
        P("tm", None, None),
        P(),
        P(),
    )
    return jax.shard_map(
        shards, mesh=mesh, in_specs=placed, out_specs=P(None, "lev", None, "tm"), check_vma=False
    )
```

profile of v0, /device:TPU:0, one launch (start us, length us, event | category | flops | bytes accessed | tf_op | source)
XLA Modules:
  0.0 140.8 jit_solution(5177221866392293401)
XLA Ops:
  0.0 0.0 copy-start
  0.0 0.7 constant_dynamic-slice_fusion.1
  0.8 0.2 reshape.39
  0.9 1.3 reshape_squeeze.6
  2.3 0.9 convert_element_type.9
  3.2 0.1 broadcast_in_dim.13
  3.3 0.7 pad_maximum_fusion
  4.0 18.5 %all_to_all.15 = f32[4,4,16384]{2,1,0:T(4,128)S(1)} all-to-all(f32[4,4,16384]{2,1,0:T(4,128)S(1)} %pad_maximum_fusion), channel_id=1, replica_groups=mesh['tm'=4,'lev'=8] {'tm'}, dimensions={0} | all-to-all | bytes 2097152 | tf_op jit(solution)/shard_map/all_to_all | solution.py:262
  22.5 4.4 %all-to-all-start.1 = ((f32[4,256,512]{2,1,0:T(8,128)}), f32[4,256,512]{2,1,0:T(8,128)}, u32[]{:S(2)}, u32[]{:S(2)}) async-start(f32[4,256,512]{2,1,0:T(8,128)} %bitcast.1), calls=%async_computation.1 | async-start | bytes 4194304 | tf_op jit(solution)/shard_map/all_to_all | solution.py:267
  27.0 1.2 fusion.1
  28.1 1.0 slice.21.innov_ref
  29.1 45.5 %shard_map.118.field_ref = f32[4,256,512]{2,1,0:T(8,128)} custom-call(s32[4,1,16384]{2,1,0:T(1,128)} %get-tuple-element.6.cell_ref, f32[4,2,16384]{2,1,0:T(2,128)} %slice.21.innov_ref), custom_call_target="tpu_custom_call" | custom-call | flops 34359738368 | bytes 8388608 | tf_op jit(solution)/shard_map/pallas_call | solution.py:88
  74.7 0.2 copy.33
  74.9 0.0 all-to-all-done.1.tangent_ref
  74.9 0.6 tile.11
  75.5 42.7 %shard_map.119 = f32[1024,128]{1,0:T(8,128)} custom-call(f32[4,256,512]{2,1,0:T(8,128)} %shard_map.118.field_ref, f32[4,256,512]{2,1,0:T(8,128)} %all-to-all-done.1.tangent_ref, f32[4,8,128]{2,1,0:T(8,128)} %bitcast.21, bf16[256,512]{1,0:T(8,128)(2,1)} %constant.33.clone.fhigh_ref, bf16[256,512]{1,0:T(8,128)(2,1)} %constant.34.clone.flow_ref, ...), custom_call_target="tpu_custom_call" | custom-call | tf_op jit(solution)/shard_map/pallas_call | solution.py:217
  118.2 1.1 slice.24
  119.3 0.4 reshape.43
  119.8 0.0 copy-start.1
  119.8 0.8 copy.28
  120.6 1.7 %reshape.46 = f32[32,2,1024]{2,1,0:T(2,128)} reshape(f32[8,4,2,16,2,32]{5,4,3,2,1,0:T(2,128)S(1)} %copy.28) | data formatting | bytes 524288 | tf_op jit(solution)/shard_map/reshape | solution.py:278
  122.3 6.3 %all-to-all-start.2 = ((f32[32,2,1024]{2,1,0:T(2,128)}), f32[32,2,1024]{2,1,0:T(2,128)S(1)}, u32[]{:S(2)}, u32[]{:S(2)}) async-start(f32[32,2,1024]{2,1,0:T(2,128)} %reshape.46), calls=%async_computation.2 | async-start | bytes 524288 | tf_op jit(solution)/shard_map/all_to_all | solution.py:279
  128.6 0.0 copy-done.1
  128.6 0.1 constant_dynamic-slice_fusion
  128.7 0.1 copy.25
  128.8 0.1 mul.19
  128.8 0.2 copy.26
  129.0 10.2 %all-to-all-done.2 = f32[32,2,1024]{2,1,0:T(2,128)S(1)} async-done(((f32[32,2,1024]{2,1,0:T(2,128)}), f32[32,2,1024]{2,1,0:T(2,128)S(1)}, u32[]{:S(2)}, u32[]{:S(2)}) %all-to-all-start.2) | async-done | bytes 262176 | tf_op jit(solution)/shard_map/all_to_all | solution.py:279
  139.2 0.2 reshape_reshape.3
  139.4 0.0 copy-done
  139.4 0.4 convolution_bitcast_fusion
  139.8 1.0 copy.27
  (6 shorter events, 0.1 us)
Async XLA Ops:
  0.0 139.4 %copy-start = (f32[64,64]{1,0:T(8,128)S(1)}, f32[64,64]{1,0:T(8,128)}, u32[]{:S(2)}) copy-start(f32[64,64]{1,0:T(8,128)} %param.17) | copy-start | bytes 49156
  22.5 52.3 %all-to-all-start.1 = ((f32[4,256,512]{2,1,0:T(8,128)}), f32[4,256,512]{2,1,0:T(8,128)}, u32[]{:S(2)}, u32[]{:S(2)}) async-start(f32[4,256,512]{2,1,0:T(8,128)} %bitcast.1), calls=%async_computation.1 | async-start | bytes 4194304 | tf_op jit(solution)/shard_map/all_to_all | solution.py:267
  119.8 8.9 %copy-start.1 = (f32[64,128]{1,0:T(8,128)S(1)}, f32[64,128]{1,0:T(8,128)}, u32[]{:S(2)}) copy-start(f32[64,128]{1,0:T(8,128)} %param.16) | copy-start | bytes 98308
  122.3 16.9 %all-to-all-start.2 = ((f32[32,2,1024]{2,1,0:T(2,128)}), f32[32,2,1024]{2,1,0:T(2,128)S(1)}, u32[]{:S(2)}, u32[]{:S(2)}) async-start(f32[32,2,1024]{2,1,0:T(2,128)} %reshape.46), calls=%async_computation.2 | async-start | bytes 524288 | tf_op jit(solution)/shard_map/all_to_all | solution.py:279
where the time goes:
time: 141 us
  Pallas kernels  88.3 us (63%)
  blocking collectives  18.5 us (13%)
  starting transfers between devices  10.8 us (8%)
  waiting for transfers between devices  10.2 us (7%)
  local copies, waits for them, and re-layouts  9.8 us (7%)
  other arithmetic  2.74 us (2%)
    pallas_call x1, Pallas kernels, forcing_fields(): pl.pallas_call(body, grid=(times, count // width), in_specs=[pl.BlockSpec...  45.5 us
    pallas_call x1, Pallas kernels, sweep(): pl.pallas_call(sweep_kernel, in_specs=[pl.BlockSpec(memory_space=pltpu.VM...  42.7 us
    all_to_all x1, blocking collectives, shards(): lax.all_to_all(message, 'tm', split_axis=0, concat_axis=0, tiled=True)  18.5 us
    all_to_all x1, waiting for transfers between devices, shards(): lax.all_to_all(outgoing, ('lev', 'tm'), split_axis=0, concat_axis=0, tile...  10.2 us
    all_to_all x1, starting transfers between devices, shards(): lax.all_to_all(outgoing, ('lev', 'tm'), split_axis=0, concat_axis=0, tile...  6.32 us
    all_to_all x1, starting transfers between devices, shards(): lax.all_to_all(pad_levels(tangent[0], 0).reshape(sections, mine * lat_row...  4.45 us
  transfers between devices with their start and end apart: 2, of which 1 were waited for; matrix products, arithmetic and copies ran while one was open for 2% of the time, Pallas kernels for 32%

commit v1 on v0

v1 whole, which is shorter than its diff:
```python
import functools
import math

import jax
import jax.numpy as jnp
import numpy as np
from jax import lax
from jax.experimental import pallas as pl
from jax.experimental.pallas import tpu as pltpu
from jax.sharding import PartitionSpec as P

PRECISE = lax.Precision.HIGHEST
BF16 = jnp.bfloat16
F32 = jnp.float32
NT = (((1,), (1,)), ((), ()))
NN = (((1,), (0,)), ((), ()))
VMEM_BYTES = 62 * 1024 * 1024
LANES = 128


def dot(left, right, dims):
    return lax.dot_general(left, right, dims, preferred_element_type=F32)


def halves(value):
    high = value.astype(BF16)
    return high, (value - high.astype(F32)).astype(BF16)


def fourier_rows(lon_count, wave_count):
    index = np.arange(wave_count)[:, None] * np.arange(lon_count)[None, :] % lon_count
    angles = 2.0 * np.pi * index / lon_count
    return (np.concatenate([np.cos(angles), np.sin(angles)], 0) * np.sqrt(2.0 / lon_count)).astype(np.float32)


def legendre_coefficients(lat_count, wave_count):
    half = lat_count // 2
    pack = 2 * LANES // half
    groups = wave_count // pack
    deep = LANES // pack
    phi = (np.arange(half) + 0.5) * np.pi / lat_count - 0.5 * np.pi
    orders = np.arange(wave_count).astype(np.float64)
    lead = np.array(
        [
            -0.5 * math.log(2.0)
            + 0.5 * (math.lgamma(m + 1.5) - math.lgamma(1.5) - math.lgamma(m + 1.0))
            for m in range(wave_count)
        ]
    )
    weight = np.sqrt(np.pi * np.cos(phi) / lat_count)
    diagonal = weight[None, :] * np.exp(lead[:, None] + orders[:, None] * np.log(np.cos(phi))[None, :])
    diagonal = diagonal.reshape(groups, pack * half)
    mu = np.broadcast_to(np.tile(np.sin(phi), pack)[None, :], (groups, pack * half))
    degree = orders[:, None]
    above = degree > orders[None, :]
    gap = np.where(above, degree**2 - orders[None, :] ** 2, 1.0)
    up = np.where(above, np.sqrt(np.maximum(4.0 * degree**2 - 1.0, 0.0) / gap), 0.0)
    lower = degree - 1.0
    down = np.sqrt(np.maximum(lower**2 - orders[None, :] ** 2, 0.0) / np.maximum(4.0 * lower**2 - 1.0, 1.0))

    def packed(a):
        a = a.reshape(wave_count // deep, deep, groups, pack)
        return a.transpose(0, 2, 1, 3).reshape(wave_count // deep * groups, deep * pack)

    return [np.asarray(a, np.float32) for a in (mu, diagonal, packed(up), packed(up * down))]


def forcing_kernel(lat_rows, lon_cols, cell_ref, innov_ref, out_ref):
    cells = cell_ref[0]
    width = cells.shape[1]
    rows = cells // lon_cols
    cols = cells - rows * lon_cols
    innov = innov_ref[0]
    levels = innov.shape[0]
    hit = lax.broadcasted_iota(jnp.int32, (lat_rows, width), 0) == rows
    spread_cols = jnp.where(
        lax.broadcasted_iota(jnp.int32, (lon_cols, width), 0) == cols, 1.0, 0.0
    ).astype(BF16)
    high = innov.astype(BF16).astype(F32)
    low = innov - high
    pieces = [jnp.where(hit, part[k : k + 1, :], 0.0).astype(BF16) for part in (high, low) for k in range(levels)]
    field = dot(jnp.concatenate(pieces, 0), spread_cols, NT)
    field = field[: levels * lat_rows] + field[levels * lat_rows :]

    @pl.when(pl.program_id(1) == 0)
    def _():
        out_ref[0] = field

    @pl.when(pl.program_id(1) > 0)
    def _():
        out_ref[0] += field


def forcing_fields(cells, innov, lat_rows, lon_cols):
    times, levels, count = innov.shape
    width = math.gcd(count, 2048)
    body = functools.partial(forcing_kernel, lat_rows, lon_cols)
    return pl.pallas_call(
        body,
        grid=(times, count // width),
        in_specs=[
            pl.BlockSpec((1, 1, width), lambda t, c: (t, 0, c)),
            pl.BlockSpec((1, levels, width), lambda t, c: (t, 0, c)),
        ],
        out_specs=pl.BlockSpec((1, levels * lat_rows, lon_cols), lambda t, c: (t, 0, 0)),
        out_shape=jax.ShapeDtypeStruct((times, levels * lat_rows, lon_cols), F32),
        compiler_params=pltpu.CompilerParams(vmem_limit_bytes=VMEM_BYTES),
        cost_estimate=pl.CostEstimate(
            flops=4 * times * levels * lat_rows * lon_cols * count, bytes_accessed=8 * 2**20, transcendentals=0
        ),
    )(cells.reshape(times, 1, count), innov)


def lanes_at(value, index):
    return jnp.take_along_axis(value, jnp.broadcast_to(index, value.shape), axis=1, mode="promise_in_bounds")


def sweep_kernel(
    sections, field_ref, tangent_ref, damp_ref, scale_ref, fhigh_ref, flow_ref, mu_ref, diag_ref, up_ref, both_ref,
    out_ref, left, right, high, low, even, odd, packed, total, adjoint, order,
):
    times, rows, lon_cols = field_ref.shape
    groups, width = mu_ref.shape
    waves = high.shape[1]
    lat_rows = width * groups * 2 // waves
    half = lat_rows // 2
    pack = width // half
    deep = LANES // pack
    levels = rows // lat_rows
    group = damp_ref.shape[1]
    mid = group // 2

    lane = lax.broadcasted_iota(jnp.int32, (1, LANES), 1)
    in_first = lane < half
    fold = lane % half
    sub = lax.broadcasted_iota(jnp.int32, (groups, width), 0)
    orders = sub * pack + lax.broadcasted_iota(jnp.int32, (groups, width), 1) // half

    def advance(n, state):
        one, two = state
        place = pl.ds(pl.multiple_of(n // deep * groups, groups), groups)
        base = (n % deep) * pack

        def spread_out(ref):
            value = ref[place, :]
            return jnp.concatenate([lanes_at(value, base + lane // half + i * (LANES // half)) for i in range(width // LANES)], 1)

        recurred = spread_out(up_ref) * (mu_ref[...] * one) - spread_out(both_ref) * two
        value = jnp.where(orders == n, diag_ref[...], recurred)
        row = (n % 2) * (waves // 2) + n // 2
        left[pl.ds(row, groups, stride=waves), :] = value[:, :LANES]
        right[pl.ds(row, groups, stride=waves), :] = value[:, LANES:]
        return value, one

    zero = 0.0 * mu_ref[...]
    lax.fori_loop(0, waves, advance, (zero, zero), unroll=8)

    def split(g, carry):
        for i, ref in enumerate((left, right)):
            upper, lower = halves(ref[pl.ds(pl.multiple_of(g * waves, waves), waves), :])
            high[g, :, i * LANES : (i + 1) * LANES] = upper
            low[g, :, i * LANES : (i + 1) * LANES] = lower
        return carry

    lax.fori_loop(0, groups, split, 0, unroll=4)

    in_high = lax.broadcasted_iota(jnp.int32, (group, LANES), 0) < mid
    n_even = lax.broadcasted_iota(jnp.int32, (group, LANES), 1) < waves // 2
    lat_south = lax.broadcasted_iota(jnp.int32, (group, LANES), 1) < half
    adjoint[...] = jnp.zeros_like(adjoint)
    total[...] = jnp.zeros_like(total)
    own_half = (lax.broadcasted_iota(jnp.int32, (waves, LANES), 1) // half) == (
        lax.broadcasted_iota(jnp.int32, (waves, LANES), 0) % (LANES // half)
    )

    def analyse(t):
        forced = adjoint[...] + field_ref[t]
        adjoint[...] = forced
        upper, lower = halves(forced)
        coeffs = dot(fhigh_ref[...], upper, NT) + dot(flow_ref[...], upper, NT) + dot(fhigh_ref[...], lower, NT)
        for k in range(levels):
            for p in range(2):
                part = coeffs[p * waves : (p + 1) * waves, k * lat_rows : (k + 1) * lat_rows]
                south = lanes_at(part, fold)
                north = lanes_at(part, lat_rows - 1 - fold)
                for value, ref in ((south + north, even), (south - north, odd)):
                    value = jnp.where(own_half, value, 0.0)
                    rounded = value.astype(BF16).astype(F32)
                    ref[pl.ds(2 * k + p, waves, stride=group), :] = rounded
                    ref[pl.ds(mid + 2 * k + p, waves, stride=group), :] = value - rounded

    def pair_sum(value):
        return value + pltpu.roll(value, mid, 0)

    blank = jnp.zeros((group, LANES), F32)
    per_tile = LANES // half

    def place_of(g, i):
        return pl.ds(pl.multiple_of((g * pack + i) * group, group), group)

    def spectral_of(g):
        lefts = []
        for i in range(pack):
            for ref in (even, odd):
                value = ref[place_of(g, i), :]
                tiles = [value if i // per_tile == c else blank for c in range(width // LANES)]
                lefts.append(jnp.concatenate(tiles, 1))
        lefts = jnp.concatenate(lefts, 0).astype(BF16)
        product = dot(lefts, high[g], NT) + dot(lefts, low[g], NT)
        values = []
        for i in range(pack):
            same = product[2 * i * group : (2 * i + 1) * group]
            other = product[(2 * i + 1) * group : (2 * i + 2) * group]
            value = pair_sum(jnp.where(n_even, same, other) if i % 2 == 0 else jnp.where(n_even, other, same))
            total[place_of(g, i), :] += value
            values.append(value)
        return values

    def synthesise(g, values, damp):
        lefts = []
        for i, value in enumerate(values):
            filtered = value * damp
            rounded = filtered.astype(BF16).astype(F32)
            parts = jnp.where(in_high, rounded, filtered - rounded)
            first, second = jnp.where(n_even, parts, 0.0), jnp.where(n_even, 0.0, parts)
            lefts += [first, second] if i % 2 == 0 else [second, first]
        lefts = jnp.concatenate(lefts, 0).astype(BF16)
        product = dot(lefts, high[g], NN) + dot(lefts, low[g], NN)
        for i in range(pack):
            tile = slice(i // per_tile * LANES, (i // per_tile + 1) * LANES)
            same = product[2 * i * group : (2 * i + 1) * group, tile]
            other = product[(2 * i + 1) * group : (2 * i + 2) * group, tile]
            index = (i % per_tile) * half + jnp.where(in_first, lane, lat_rows - 1 - lane)
            same, other = lanes_at(same, index), lanes_at(other, index)
            packed[place_of(g, i), :] = pair_sum(jnp.where(lat_south, same + other, same - other))

    def step(s, carry):
        t = times - 1 - s
        analyse(t)
        damp = damp_ref[t]

        def wave(g, inner):
            synthesise(g, spectral_of(g), damp)
            return inner

        lax.fori_loop(0, groups, wave, 0, unroll=4)
        synth = jnp.concatenate(
            [
                jnp.concatenate([packed[pl.ds(2 * k + p, waves, stride=group), :] for p in range(2)], 0).T
                for k in range(levels)
            ],
            0,
        )
        upper, lower = halves(synth)
        gridded = dot(upper, fhigh_ref[...], NN) + dot(lower, fhigh_ref[...], NN) + dot(upper, flow_ref[...], NN)
        adjoint[...] = tangent_ref[t] * adjoint[...] + gridded
        return carry

    lax.fori_loop(0, times - 1, step, 0)
    analyse(0)

    def last(g, inner):
        spectral_of(g)
        return inner

    lax.fori_loop(0, groups, last, 0, unroll=4)

    block_n = waves // sections
    side = LANES // block_n
    deal = 2 * waves // side
    natural = (lane % 2) * (waves // 2) + lane // 2
    for k in range(levels):
        for p in range(2):
            value = total[pl.ds(2 * k + p, waves, stride=group), :]
            order[pl.ds(p, waves, stride=2), :] = lanes_at(value, natural) * scale_ref[k : k + 1, :]
        blocks = [order[pl.ds(q, deal, stride=side), :] for q in range(side)]
        for s in range(sections):
            value = blocks[0] if s == 0 else pltpu.roll(blocks[0], (-s * block_n) % LANES, 1)
            for q in range(1, side):
                moved = blocks[q] if q == s else pltpu.roll(blocks[q], ((q - s) * block_n) % LANES, 1)
                value = jnp.where(lane // block_n == q, moved, value)
            out_ref[s * levels + k] = value


def sweep(fields, tangent, damp, scale, lat_rows, waves, sections):
    times, rows, lon_cols = fields.shape
    group = damp.shape[1]
    levels = rows // lat_rows
    fourier = fourier_rows(lon_cols, waves)
    fhigh = fourier.astype(jnp.bfloat16)
    flow = (fourier - fhigh.astype(np.float32)).astype(jnp.bfloat16)
    mu, diagonal, up, both = legendre_coefficients(lat_rows, waves)
    groups, width = mu.shape
    return pl.pallas_call(
        functools.partial(sweep_kernel, sections),
        in_specs=[pl.BlockSpec(memory_space=pltpu.VMEM)] * 10,
        out_specs=pl.BlockSpec(memory_space=pltpu.VMEM),
        out_shape=jax.ShapeDtypeStruct((sections * levels, 2 * waves * (waves // sections) // LANES, LANES), F32),
        scratch_shapes=[
            pltpu.VMEM((waves * groups, LANES), F32),
            pltpu.VMEM((waves * groups, LANES), F32),
            pltpu.VMEM((groups, waves, width), BF16),
            pltpu.VMEM((groups, waves, width), BF16),
            pltpu.VMEM((waves * group, LANES), F32),
            pltpu.VMEM((waves * group, LANES), F32),
            pltpu.VMEM((waves * group, LANES), F32),
            pltpu.VMEM((waves * group, LANES), F32),
            pltpu.VMEM((rows, lon_cols), F32),
            pltpu.VMEM((2 * waves, LANES), F32),
        ],
        compiler_params=pltpu.CompilerParams(vmem_limit_bytes=VMEM_BYTES),
    )(fields, tangent, damp, scale, fhigh, flow, mu, diagonal, up, both)


def shards(obs_cell, innovation, tangent, damping, spread, vertical):
    sections = lax.axis_size("tm")
    groups = lax.axis_size("lev")
    me_tm = lax.axis_index("tm")
    me_lev = lax.axis_index("lev")
    lev_dev, lat_rows, lon_cols = tangent.shape[1:]
    levels, waves = damping.shape[1:]
    mine = -(-lev_dev // sections)
    mine += mine % 2
    padded = mine * sections

    def pad_levels(value, axis):
        widths = [(0, 0)] * value.ndim
        widths[axis] = (0, padded - value.shape[axis])
        return jnp.pad(value, widths) if padded > value.shape[axis] else value

    count = obs_cell.shape[1]
    deep = count // LANES
    damp_block = pad_levels(lax.dynamic_slice_in_dim(damping[0], me_lev * lev_dev, lev_dev, 0), 0)
    message = jnp.concatenate(
        [
            pad_levels(innovation[0], 0).reshape(sections, mine * deep, LANES),
            jnp.broadcast_to(obs_cell.astype(F32).reshape(1, deep, LANES), (sections, deep, LANES)),
            damp_block.reshape(sections, mine * waves // LANES, LANES),
        ],
        1,
    )
    message = lax.all_to_all(message, "tm", split_axis=0, concat_axis=0, tiled=True)
    innov = message[:, : mine * deep].reshape(sections, mine, count)
    cells = message[:, mine * deep : (mine + 1) * deep].reshape(sections, count).astype(jnp.int32)
    damp_mine = message[:, (mine + 1) * deep :].reshape(sections, mine, waves)
    rates = lax.all_to_all(
        pad_levels(tangent[0], 0).reshape(sections, mine * lat_rows, lon_cols),
        "tm", split_axis=0, concat_axis=0, tiled=True,
    )
    fields = forcing_fields(cells, innov, lat_rows, lon_cols)
    damp_mine = jnp.concatenate([damp_mine[..., 0::2], damp_mine[..., 1::2]], -1)
    damp_rows = jnp.tile(jnp.repeat(damp_mine, 2, axis=1), (1, 2, 1))
    scale = pad_levels(lax.dynamic_slice_in_dim(spread, me_lev * lev_dev, lev_dev, 0), 0)
    scale = lax.dynamic_slice_in_dim(scale, me_tm * mine, mine, 0)
    total = sweep(fields, rates, damp_rows, scale, lat_rows, waves, sections)

    block_m = waves // groups
    block_n = waves // sections
    deal = total.shape[1] // groups
    outgoing = total.reshape(sections, mine, groups, deal, LANES)
    outgoing = outgoing.transpose(2, 0, 1, 3, 4).reshape(groups * sections, mine * deal, LANES)
    arrived = lax.all_to_all(outgoing, ("lev", "tm"), split_axis=0, concat_axis=0, tiled=True)
    arrived = arrived.reshape(groups, padded, deal * LANES)[:, :lev_dev].reshape(levels, deal * LANES)
    result = jnp.einsum("kj,kx->jx", vertical, arrived, precision=PRECISE)
    return result.reshape(levels, block_m, 2, block_n)


def solution(mesh):
    placed = (
        P("tm", None),
        P("tm", "lev", None),
        P("tm", "lev", None, None),
        P("tm", None, None),
        P(),
        P(),
    )
    return jax.shard_map(
        shards, mesh=mesh, in_specs=placed, out_specs=P(None, "lev", None, "tm"), check_vma=False
    )
```

time: 141 us -> 135 us (0.957)
  local copies, waits for them, and re-layouts: 9.8 us -> 7.22 us
  starting transfers between devices: 10.8 us -> 8.72 us
    all_to_all x1, starting transfers between devices: 6.32 us -> 4.26 us  [shards(): lax.all_to_all(message, 'tm', split_axis=0, concat_axis=0, tiled=True)]
    slice x3 -> x4, local copies, waits for them, and re-layouts: 2.05 us -> 0.36 us  [the longest x1 0.16 us: shards(): damp_mine[..., 1::2]]
    reshape x6 -> x2, local copies, waits for them, and re-layouts: 3.15 us -> 2.08 us  [the longest x1 1.11 us: shards(): innov = message[:, :mine * deep].reshape(sections, mine, count)]
  transfers between devices with their start and end apart: 2 -> 2, of which waited for: 1 -> 1; matrix products, arithmetic and copies ran while one was open for 2% -> 3% of each run, Pallas kernels for 32% -> 34%
where the time goes in v1:
time: 135 us
  Pallas kernels  87.8 us (65%)
  blocking collectives  17.4 us (13%)
  waiting for transfers between devices  10.5 us (8%)
  starting transfers between devices  8.72 us (6%)
  local copies, waits for them, and re-layouts  7.22 us (5%)
  other arithmetic  2.64 us (2%)
    pallas_call x1, Pallas kernels, forcing_fields(): pl.pallas_call(body, grid=(times, count // width), in_specs=[pl.BlockSpec...  45.5 us
    pallas_call x1, Pallas kernels, sweep(): pl.pallas_call(functools.partial(sweep_kernel, sections), in_specs=[pl.Bl...  42.2 us
    all_to_all x1, blocking collectives, shards(): lax.all_to_all(outgoing, ('lev', 'tm'), split_axis=0, concat_axis=0, tile...  17.4 us
    all_to_all x1, waiting for transfers between devices, shards(): lax.all_to_all(message, 'tm', split_axis=0, concat_axis=0, tiled=True)  10.5 us
    all_to_all x1, starting transfers between devices, shards(): lax.all_to_all(pad_levels(tangent[0], 0).reshape(sections, mine * lat_row...  4.45 us
    all_to_all x1, starting transfers between devices, shards(): lax.all_to_all(message, 'tm', split_axis=0, concat_axis=0, tiled=True)  4.26 us
  transfers between devices with their start and end apart: 2, of which 1 were waited for; matrix products, arithmetic and copies ran while one was open for 3% of the time, Pallas kernels for 34%

profile of v1, /device:TPU:0, one launch (start us, length us, event | category | flops | bytes accessed | tf_op | source)
XLA Modules:
  0.0 134.7 jit_solution(1045245465247156664)
XLA Ops:
  0.0 0.0 copy-start
  0.0 1.1 reshape_squeeze.6
  1.1 0.9 convert_element_type.16
  2.0 0.7 constant_dynamic-slice_fusion.1
  2.7 1.0 pad_maximum_fusion
  3.7 4.3 %all-to-all-start = ((f32[4,386,128]{2,1,0:T(8,128)}), f32[4,386,128]{2,1,0:T(8,128)S(1)}, u32[]{:S(2)}, u32[]{:S(2)}) async-start(f32[4,386,128]{2,1,0:T(8,128)} %pad_maximum_fusion), calls=%async_computation | async-start | bytes 1605632 | tf_op jit(solution)/shard_map/all_to_all | solution.py:342
  8.0 1.3 constant_dynamic-slice_fusion.scale_ref
  9.2 10.5 %all-to-all-done = f32[4,386,128]{2,1,0:T(8,128)S(1)} async-done(((f32[4,386,128]{2,1,0:T(8,128)}), f32[4,386,128]{2,1,0:T(8,128)S(1)}, u32[]{:S(2)}, u32[]{:S(2)}) %all-to-all-start) | async-done | bytes 790560 | tf_op jit(solution)/shard_map/all_to_all | solution.py:342
  19.8 4.5 %all-to-all-start.1 = ((f32[4,256,512]{2,1,0:T(8,128)}), f32[4,256,512]{2,1,0:T(8,128)}, u32[]{:S(2)}, u32[]{:S(2)}) async-start(f32[4,256,512]{2,1,0:T(8,128)} %bitcast.15), calls=%async_computation.1 | async-start | bytes 4194304 | tf_op jit(solution)/shard_map/all_to_all | solution.py:346
  24.3 1.1 reshape.37.innov_ref
  25.4 0.7 slice_convert_fusion
  26.1 45.5 %shard_map.118.field_ref = f32[4,256,512]{2,1,0:T(8,128)} custom-call(s32[4,1,16384]{2,1,0:T(1,128)} %bitcast.19, f32[4,2,16384]{2,1,0:T(2,128)} %reshape.37.innov_ref), custom_call_target="tpu_custom_call" | custom-call | flops 34359738368 | bytes 8388608 | tf_op jit(solution)/shard_map/pallas_call | solution.py:98
  71.6 0.2 slice.18
  71.8 0.2 slice.19
  72.0 0.1 pad_maximum_fusion.1
  72.0 0.0 all-to-all-done.1.tangent_ref
  72.1 0.6 tile.11
  72.7 42.2 %shard_map.119 = f32[8,64,128]{2,1,0:T(8,128)} custom-call(f32[4,256,512]{2,1,0:T(8,128)} %shard_map.118.field_ref, f32[4,256,512]{2,1,0:T(8,128)} %all-to-all-done.1.tangent_ref, f32[4,8,128]{2,1,0:T(8,128)} %bitcast.20, f32[2,128]{1,0:T(2,128)} %constant_dynamic-slice_fusion.scale_ref, bf16[256,512]{1,0:T(8,128)(2,1)} %constant.40.clone.fhigh_ref, ...), custom_call_target="tpu_custom_call" | custom-call | tf_op jit(solution)/shard_map/pallas_call | solution.py:294
  114.9 1.0 copy.14
  115.9 17.4 %all_to_all.15 = f32[32,16,128]{2,1,0:T(8,128)S(1)} all-to-all(f32[32,16,128]{2,1,0:T(8,128)S(1)} %bitcast.17), channel_id=1, replica_groups=mesh['tm'=4,'lev'=8] {'lev','tm'}, dimensions={0} | all-to-all | bytes 524288 | tf_op jit(solution)/shard_map/all_to_all | solution.py:362
  133.3 0.0 copy-done
  133.3 0.4 convolution_bitcast_fusion
  133.7 1.0 copy.15
  (5 shorter events, 0.1 us)
Async XLA Ops:
  0.0 133.3 %copy-start = (f32[64,64]{1,0:T(8,128)S(1)}, f32[64,64]{1,0:T(8,128)}, u32[]{:S(2)}) copy-start(f32[64,64]{1,0:T(8,128)} %param.17) | copy-start | bytes 49156
  3.7 16.1 %all-to-all-start = ((f32[4,386,128]{2,1,0:T(8,128)}), f32[4,386,128]{2,1,0:T(8,128)S(1)}, u32[]{:S(2)}, u32[]{:S(2)}) async-start(f32[4,386,128]{2,1,0:T(8,128)} %pad_maximum_fusion), calls=%async_computation | async-start | bytes 1605632 | tf_op jit(solution)/shard_map/all_to_all | solution.py:342
  19.8 52.3 %all-to-all-start.1 = ((f32[4,256,512]{2,1,0:T(8,128)}), f32[4,256,512]{2,1,0:T(8,128)}, u32[]{:S(2)}, u32[]{:S(2)}) async-start(f32[4,256,512]{2,1,0:T(8,128)} %bitcast.15), calls=%async_computation.1 | async-start | bytes 4194304 | tf_op jit(solution)/shard_map/all_to_all | solution.py:346

commit v2 on v1

--- a/solution.py
+++ b/solution.py
@@ -16,6 +16,7 @@
 NN = (((1,), (0,)), ((), ()))
 VMEM_BYTES = 62 * 1024 * 1024
 LANES = 128
+SUBLANES = 8
 
 
 def dot(left, right, dims):
@@ -65,50 +66,213 @@
     return [np.asarray(a, np.float32) for a in (mu, diagonal, packed(up), packed(up * down))]
 
 
-def forcing_kernel(lat_rows, lon_cols, cell_ref, innov_ref, out_ref):
-    cells = cell_ref[0]
-    width = cells.shape[1]
-    rows = cells // lon_cols
-    cols = cells - rows * lon_cols
-    innov = innov_ref[0]
-    levels = innov.shape[0]
-    hit = lax.broadcasted_iota(jnp.int32, (lat_rows, width), 0) == rows
-    spread_cols = jnp.where(
-        lax.broadcasted_iota(jnp.int32, (lon_cols, width), 0) == cols, 1.0, 0.0
-    ).astype(BF16)
-    high = innov.astype(BF16).astype(F32)
-    low = innov - high
-    pieces = [jnp.where(hit, part[k : k + 1, :], 0.0).astype(BF16) for part in (high, low) for k in range(levels)]
-    field = dot(jnp.concatenate(pieces, 0), spread_cols, NT)
-    field = field[: levels * lat_rows] + field[levels * lat_rows :]
-
-    @pl.when(pl.program_id(1) == 0)
-    def _():
-        out_ref[0] = field
-
-    @pl.when(pl.program_id(1) > 0)
-    def _():
-        out_ref[0] += field
-
-
-def forcing_fields(cells, innov, lat_rows, lon_cols):
-    times, levels, count = innov.shape
-    width = math.gcd(count, 2048)
-    body = functools.partial(forcing_kernel, lat_rows, lon_cols)
+def bin_shape(lat_rows, lon_cols):
+    tall = math.gcd(lat_rows, 32)
+    return tall, (lat_rows // tall) * (lon_cols // LANES)
+
+
+def sort_kernel(
+    lon_cols, tall, bins, mine, cell_ref, innov_ref, damp_ref, out_ref, lane_from, sub_from, swaps,
+):
+    levels, deep, _ = innov_ref.shape
+    sections = out_ref.shape[0]
+    blocks = deep // SUBLANES
+    low_bits, mid_bits, top_bits = (n.bit_length() - 1 for n in (blocks, SUBLANES, LANES))
+    mid_end = low_bits + mid_bits
+    all_bits = mid_end + top_bits
+    lane = lax.broadcasted_iota(jnp.int32, (SUBLANES, LANES), 1)
+    sub = lax.broadcasted_iota(jnp.int32, (SUBLANES, LANES), 0)
+    span = tall * LANES
+    wide = lon_cols // LANES
+
+    def key_of(cells):
+        rows = cells // lon_cols
+        cols = cells - rows * lon_cols
+        tile = (rows // tall) * wide + cols // LANES
+        return tile * span + (rows % tall) * LANES + cols % LANES
+
+    keys = [key_of(cell_ref[v * SUBLANES : (v + 1) * SUBLANES, :]) for v in range(blocks)]
+
+    def falling(stage):
+        if stage >= all_bits:
+            return None
+        if stage >= mid_end:
+            return (lane >> (stage - mid_end)) & 1
+        return (sub >> (stage - low_bits)) & 1
+
+    plan = []
+
+    def across(values, bits, position, axis, stage, first, last):
+        down = falling(stage)
+        values = [value * (1 << bits) + position for value in values]
+        for bit in range(first, last - 1, -1):
+            reach = 1 << bit
+            index = position ^ reach
+            upper = (position >> bit) & 1
+            keep = (upper if down is None else upper ^ down) == 0
+            moved = []
+            for value in values:
+                other = jnp.take_along_axis(value, index, axis=axis, mode="promise_in_bounds")
+                moved.append(jnp.where(keep, jnp.minimum(value, other), jnp.maximum(value, other)))
+            values = moved
+        return [value >> bits for value in values], [value & ((1 << bits) - 1) for value in values]
+
+    for stage in range(1, all_bits + 1):
+        if stage > mid_end:
+            keys, source = across(keys, top_bits, lane, 1, stage, stage - 1 - mid_end, 0)
+            slot = sum(1 for kind, _ in plan if kind == "lane")
+            for v in range(blocks):
+                lane_from[slot, v] = source[v]
+            plan.append(("lane", slot))
+        if stage > low_bits:
+            keys, source = across(keys, mid_bits, sub, 0, stage, min(stage, mid_end) - 1 - low_bits, 0)
+            slot = sum(1 for kind, _ in plan if kind == "sub")
+            for v in range(blocks):
+                sub_from[slot, v] = source[v]
+            plan.append(("sub", slot))
+        for bit in range(min(stage, low_bits) - 1, -1, -1):
+            down = None if stage < low_bits else falling(stage)
+            slot = sum(1 for kind, _ in plan if kind == "swap")
+            pair = 0
+            for v in range(blocks):
+                if v >> bit & 1:
+                    continue
+                first, second = keys[v], keys[v | 1 << bit]
+                if stage < low_bits:
+                    swap = first < second if v >> stage & 1 else first > second
+                elif down is None:
+                    swap = first > second
+                else:
+                    swap = jnp.where(down == 0, first - second, second - first) > 0
+                swaps[slot, pair] = jnp.where(swap, 1, 0)
+                keys[v], keys[v | 1 << bit] = jnp.where(swap, second, first), jnp.where(swap, first, second)
+                pair += 1
+            plan.append(("swap", (slot, bit)))
+
+    for s in range(sections):
+        out_ref[s, mine * deep : (mine + 1) * deep, :] = jnp.concatenate([key.astype(F32) for key in keys], 0).T
+
+    edges = jnp.zeros((1, LANES), F32)
+    for b in range(1, bins + 1):
+        below = sum(jnp.where(key < b * span, 1.0, 0.0) for key in keys)
+        below = jnp.sum(jnp.sum(below, 0, keepdims=True), 1, keepdims=True)
+        edges = jnp.where(lane[:1] == b, below, edges)
+    extra = damp_ref.shape[1]
+    base = (mine + 1) * deep
+    for s in range(sections):
+        tail = [damp_ref[s], edges, jnp.zeros((SUBLANES - extra - 1, LANES), F32)]
+        out_ref[s, base : base + SUBLANES, :] = jnp.concatenate(tail, 0)
+        for k in range(mine):
+            if s * mine + k >= levels:
+                out_ref[s, k * deep : (k + 1) * deep, :] = jnp.zeros((deep, LANES), F32)
+
+    def move(p, carry):
+        values = [innov_ref[p, v * SUBLANES : (v + 1) * SUBLANES, :] for v in range(blocks)]
+        for kind, slot in plan:
+            if kind == "swap":
+                slot, bit = slot
+                firsts = [v for v in range(blocks) if not v >> bit & 1]
+                for pair, v in enumerate(firsts):
+                    swap = swaps[slot, pair] != 0
+                    first, second = values[v], values[v | 1 << bit]
+                    values[v] = jnp.where(swap, second, first)
+                    values[v | 1 << bit] = jnp.where(swap, first, second)
+            else:
+                ref, axis = (lane_from, 1) if kind == "lane" else (sub_from, 0)
+                values = [
+                    jnp.take_along_axis(value, ref[slot, v], axis=axis, mode="promise_in_bounds")
+                    for v, value in enumerate(values)
+                ]
+        out_ref[p // mine, pl.ds(pl.multiple_of(p % mine * deep, deep), deep), :] = jnp.concatenate(values, 0).T
+        return carry
+
+    lax.fori_loop(0, levels, move, 0)
+
+
+def sorted_message(cells, innov, damp, mine, lat_rows, lon_cols):
+    levels, deep, _ = innov.shape
+    sections, extra, _ = damp.shape
+    blocks = deep // SUBLANES
+    low_bits, mid_bits, top_bits = (n.bit_length() - 1 for n in (blocks, SUBLANES, LANES))
+    all_bits = low_bits + mid_bits + top_bits
+    tall, bins = bin_shape(lat_rows, lon_cols)
+    swap_count = sum(min(stage, low_bits) for stage in range(1, all_bits + 1))
     return pl.pallas_call(
-        body,
-        grid=(times, count // width),
-        in_specs=[
-            pl.BlockSpec((1, 1, width), lambda t, c: (t, 0, c)),
-            pl.BlockSpec((1, levels, width), lambda t, c: (t, 0, c)),
+        functools.partial(sort_kernel, lon_cols, tall, bins, mine),
+        in_specs=[pl.BlockSpec(memory_space=pltpu.VMEM)] * 3,
+        out_specs=pl.BlockSpec(memory_space=pltpu.VMEM),
+        out_shape=jax.ShapeDtypeStruct((sections, (mine + 1) * deep + SUBLANES, LANES), F32),
+        scratch_shapes=[
+            pltpu.VMEM((top_bits, blocks, SUBLANES, LANES), jnp.int32),
+            pltpu.VMEM((top_bits + mid_bits, blocks, SUBLANES, LANES), jnp.int32),
+            pltpu.VMEM((swap_count, max(1, blocks // 2), SUBLANES, LANES), jnp.int32),
         ],
-        out_specs=pl.BlockSpec((1, levels * lat_rows, lon_cols), lambda t, c: (t, 0, 0)),
-        out_shape=jax.ShapeDtypeStruct((times, levels * lat_rows, lon_cols), F32),
-        compiler_params=pltpu.CompilerParams(vmem_limit_bytes=VMEM_BYTES),
-        cost_estimate=pl.CostEstimate(
-            flops=4 * times * levels * lat_rows * lon_cols * count, bytes_accessed=8 * 2**20, transcendentals=0
-        ),
-    )(cells.reshape(times, 1, count), innov)
+        compiler_params=pltpu.CompilerParams(vmem_limit_bytes=VMEM_BYTES // 2),
+        cost_estimate=pl.CostEstimate(flops=2**30, bytes_accessed=2**21, transcendentals=0),
+    )(cells, innov, damp)
+
+
+def forcing_kernel(mine, tall, edge_ref, message_ref, out_ref):
+    times = message_ref.shape[0]
+    bins = out_ref.shape[1]
+    deep = (message_ref.shape[1] - SUBLANES) // (mine + 1)
+    chunks = deep // 2
+    span = tall * LANES
+    stride = edge_ref.shape[0] // times
+    out_ref[...] = jnp.zeros_like(out_ref)
+    col_ids = lax.broadcasted_iota(jnp.int32, (LANES, 2 * LANES), 0).astype(F32).astype(BF16)
+    row_ids = lax.broadcasted_iota(jnp.int32, (tall, 2 * LANES), 0).astype(F32).astype(BF16)
+    one, none = jnp.ones((), BF16), jnp.zeros((), BF16)
+
+    def row_of(t, base, c):
+        return jnp.concatenate([message_ref[t, pl.ds(base + 2 * c + i, 1), :] for i in range(2)], 1)
+
+    def visit(t, b, c, live):
+        key = row_of(t, mine * deep, c).astype(jnp.int32) - jnp.where(live, b, bins + 1) * span
+        cols = (key & (LANES - 1)).astype(F32).astype(BF16)
+        rows = (key >> 7).astype(F32).astype(BF16)
+        spread_cols = jnp.where(col_ids == jnp.broadcast_to(cols, col_ids.shape), one, none)
+        hit = row_ids == jnp.broadcast_to(rows, row_ids.shape)
+        parts = [halves(row_of(t, k * deep, c)) for k in range(mine)]
+        pieces = [jnp.where(hit, jnp.broadcast_to(part[i], row_ids.shape), none) for i in range(2) for part in parts]
+        field = dot(jnp.concatenate(pieces, 0), spread_cols, NT)
+        return field[: mine * tall] + field[mine * tall :]
+
+    total = chunks + bins - 1
+    unroll = 4
+
+    def walk(s, state):
+        fields, nexts = [], []
+        for t in range(times):
+            b, c = state[t]
+            for u in range(unroll):
+                live = s * unroll + u < total
+                fields.append((t, b, visit(t, b, c, live)))
+                stay = edge_ref[t * stride + b + 1] > (c + 1) * 2 * LANES
+                b, c = (
+                    jnp.minimum(jnp.where(stay, b, b + 1), bins - 1),
+                    jnp.minimum(jnp.where(stay, c + 1, c), chunks - 1),
+                )
+            nexts.append((b, c))
+        for t, b, field in fields:
+            out_ref[t, b] += field
+        return tuple(nexts)
+
+    start = jnp.int32(0)
+    lax.fori_loop(0, -(-total // unroll), walk, tuple((start, start) for _ in range(times)))
+
+
+def forcing_fields(message, edges, mine, lat_rows, lon_cols):
+    times = message.shape[0]
+    tall, bins = bin_shape(lat_rows, lon_cols)
+    return pl.pallas_call(
+        functools.partial(forcing_kernel, mine, tall),
+        in_specs=[pl.BlockSpec(memory_space=pltpu.SMEM), pl.BlockSpec(memory_space=pltpu.VMEM)],
+        out_specs=pl.BlockSpec(memory_space=pltpu.VMEM),
+        out_shape=jax.ShapeDtypeStruct((times, bins, mine * tall, LANES), F32),
+        compiler_params=pltpu.CompilerParams(vmem_limit_bytes=VMEM_BYTES // 2),
+        cost_estimate=pl.CostEstimate(flops=2**33, bytes_accessed=2**22, transcendentals=0),
+    )(edges, message)
 
 
 def lanes_at(value, index):
@@ -119,7 +283,8 @@
     sections, field_ref, tangent_ref, damp_ref, scale_ref, fhigh_ref, flow_ref, mu_ref, diag_ref, up_ref, both_ref,
     out_ref, left, right, high, low, even, odd, packed, total, adjoint, order,
 ):
-    times, rows, lon_cols = field_ref.shape
+    times, rows, lon_cols = tangent_ref.shape
+    bins = field_ref.shape[1]
     groups, width = mu_ref.shape
     waves = high.shape[1]
     lat_rows = width * groups * 2 // waves
@@ -127,6 +292,8 @@
     pack = width // half
     deep = LANES // pack
     levels = rows // lat_rows
+    tall = field_ref.shape[2] // levels
+    across = lon_cols // LANES
     group = damp_ref.shape[1]
     mid = group // 2
 
@@ -174,7 +341,12 @@
     )
 
     def analyse(t):
-        forced = adjoint[...] + field_ref[t]
+        field = [
+            jnp.concatenate([field_ref[t, h + i, k * tall : (k + 1) * tall, :] for i in range(across)], 1)
+            for k in range(levels)
+            for h in range(0, bins, across)
+        ]
+        forced = adjoint[...] + jnp.concatenate(field, 0)
         adjoint[...] = forced
         upper, lower = halves(forced)
         coeffs = dot(fhigh_ref[...], upper, NT) + dot(flow_ref[...], upper, NT) + dot(fhigh_ref[...], lower, NT)
@@ -240,10 +412,16 @@
         damp = damp_ref[t]
 
         def wave(g, inner):
-            synthesise(g, spectral_of(g), damp)
+            for i, value in enumerate(spectral_of(g)):
+                packed[place_of(g, i), :] = value
             return inner
 
-        lax.fori_loop(0, groups, wave, 0, unroll=4)
+        def back(g, inner):
+            synthesise(g, [packed[place_of(g, i), :] for i in range(pack)], damp)
+            return inner
+
+        lax.fori_loop(0, groups, wave, 0, unroll=32)
+        lax.fori_loop(0, groups, back, 0, unroll=32)
         synth = jnp.concatenate(
             [
                 jnp.concatenate([packed[pl.ds(2 * k + p, waves, stride=group), :] for p in range(2)], 0).T
@@ -263,7 +441,7 @@
         spectral_of(g)
         return inner
 
-    lax.fori_loop(0, groups, last, 0, unroll=4)
+    lax.fori_loop(0, groups, last, 0, unroll=32)
 
     block_n = waves // sections
     side = LANES // block_n
@@ -283,7 +461,7 @@
 
 
 def sweep(fields, tangent, damp, scale, lat_rows, waves, sections):
-    times, rows, lon_cols = fields.shape
+    times, rows, lon_cols = tangent.shape
     group = damp.shape[1]
     levels = rows // lat_rows
     fourier = fourier_rows(lon_cols, waves)
@@ -331,23 +509,24 @@
     count = obs_cell.shape[1]
     deep = count // LANES
     damp_block = pad_levels(lax.dynamic_slice_in_dim(damping[0], me_lev * lev_dev, lev_dev, 0), 0)
-    message = jnp.concatenate(
-        [
-            pad_levels(innovation[0], 0).reshape(sections, mine * deep, LANES),
-            jnp.broadcast_to(obs_cell.astype(F32).reshape(1, deep, LANES), (sections, deep, LANES)),
-            damp_block.reshape(sections, mine * waves // LANES, LANES),
-        ],
-        1,
+    message = sorted_message(
+        obs_cell.reshape(deep, LANES),
+        innovation.reshape(lev_dev, deep, LANES),
+        damp_block.reshape(sections, mine * waves // LANES, LANES),
+        mine,
+        lat_rows,
+        lon_cols,
     )
     message = lax.all_to_all(message, "tm", split_axis=0, concat_axis=0, tiled=True)
-    innov = message[:, : mine * deep].reshape(sections, mine, count)
-    cells = message[:, mine * deep : (mine + 1) * deep].reshape(sections, count).astype(jnp.int32)
-    damp_mine = message[:, (mine + 1) * deep :].reshape(sections, mine, waves)
+    base = (mine + 1) * deep
+    extra = mine * waves // LANES
+    damp_mine = message[:, base : base + extra].reshape(sections, mine, waves)
+    edges = message[:, base + extra].astype(jnp.int32).reshape(sections * LANES)
     rates = lax.all_to_all(
         pad_levels(tangent[0], 0).reshape(sections, mine * lat_rows, lon_cols),
         "tm", split_axis=0, concat_axis=0, tiled=True,
     )
-    fields = forcing_fields(cells, innov, lat_rows, lon_cols)
+    fields = forcing_fields(message, edges, mine, lat_rows, lon_cols)
     damp_mine = jnp.concatenate([damp_mine[..., 0::2], damp_mine[..., 1::2]], -1)
     damp_rows = jnp.tile(jnp.repeat(damp_mine, 2, axis=1), (1, 2, 1))
     scale = pad_levels(lax.dynamic_slice_in_dim(spread, me_lev * lev_dev, lev_dev, 0), 0)

time: 135 us -> 101 us (0.75)
  Pallas kernels: 87.8 us -> 43.9 us
  blocking collectives: 17.4 us -> 31.1 us
  starting transfers between devices: 8.72 us -> 4.45 us
  other arithmetic: 2.64 us -> 0.08 us
  waiting for transfers between devices: 10.5 us -> 12.8 us
    pallas_call x1 -> x2, Pallas kernels: 45.5 us -> 20.7 us  [the longest x1 10.8 us: sorted_message(): pl.pallas_call(functools.partial(sort_kernel, lon_cols, tall, bins, mine)...]
    pallas_call x1, Pallas kernels: 42.2 us -> 23.1 us  [sweep(): pl.pallas_call(functools.partial(sweep_kernel, sections), in_specs=[pl.Bl...]
    all_to_all x0 -> x1, blocking collectives: none -> 15.9 us  [shards(): lax.all_to_all(message, 'tm', split_axis=0, concat_axis=0, tiled=True)]
    all_to_all x1, waiting for transfers between devices: 0.01 us -> 12.8 us  [shards(): lax.all_to_all(pad_levels(tangent[0], 0).reshape(sections, mine * lat_row...]
    all_to_all x1 -> x0, waiting for transfers between devices: 10.5 us -> none  [shards(): lax.all_to_all(message, 'tm', split_axis=0, concat_axis=0, tiled=True)]
    all_to_all x1 -> x0, starting transfers between devices: 4.26 us -> none  [shards(): lax.all_to_all(message, 'tm', split_axis=0, concat_axis=0, tiled=True)]
    unnamed x2 -> x7, local copies, waits for them, and re-layouts: 0.01 us -> 3.29 us
    all_to_all x1, blocking collectives: 17.4 us -> 15.3 us  [shards(): lax.all_to_all(outgoing, ('lev', 'tm'), split_axis=0, concat_axis=0, tile...]
  transfers between devices with their start and end apart: 2 -> 1, of which waited for: 1 -> 1; matrix products, arithmetic and copies ran while one was open for 3% -> 2% of each run, Pallas kernels for 34% -> 10%
where the time goes in v2:
time: 101 us
  Pallas kernels  43.9 us (43%)
  blocking collectives  31.1 us (31%)
  waiting for transfers between devices  12.8 us (13%)
  local copies, waits for them, and re-layouts  8.18 us (8%)
  starting transfers between devices  4.45 us (4%)
    pallas_call x1, Pallas kernels, sweep(): pl.pallas_call(functools.partial(sweep_kernel, sections), in_specs=[pl.Bl...  23.1 us
    all_to_all x1, blocking collectives, shards(): lax.all_to_all(message, 'tm', split_axis=0, concat_axis=0, tiled=True)  15.9 us
    all_to_all x1, blocking collectives, shards(): lax.all_to_all(outgoing, ('lev', 'tm'), split_axis=0, concat_axis=0, tile...  15.3 us
    all_to_all x1, waiting for transfers between devices, shards(): lax.all_to_all(pad_levels(tangent[0], 0).reshape(sections, mine * lat_row...  12.8 us
    pallas_call x1, Pallas kernels, sorted_message(): pl.pallas_call(functools.partial(sort_kernel, lon_cols, tall, bins, mine)...  10.8 us
    pallas_call x1, Pallas kernels, forcing_fields(): pl.pallas_call(functools.partial(forcing_kernel, mine, tall), in_specs=[p...  9.89 us
    all_to_all x1, starting transfers between devices, shards(): lax.all_to_all(pad_levels(tangent[0], 0).reshape(sections, mine * lat_row...  4.45 us
    unnamed x7, local copies, waits for them, and re-layouts  3.29 us
  transfers between devices with their start and end apart: 1, of which 1 were waited for; matrix products, arithmetic and copies ran while one was open for 2% of the time, Pallas kernels for 10%

profile of v2, /device:TPU:0, one launch (start us, length us, event | category | flops | bytes accessed | tf_op | source)
XLA Modules:
  0.0 101.0 jit_solution(11054832178756959957)
XLA Ops:
  0.0 0.0 copy-start
  0.0 1.2 %copy.18 = f32[1,8,128,128]{3,2,1,0:T(8,128)S(1)} copy(f32[1,8,128,128]{3,1,2,0:T(8,128)} %bitcast.26) | data formatting | bytes 1048576
  1.2 0.7 constant_dynamic-slice_fusion.1
  1.9 0.0 copy-start.2
  1.9 0.8 copy-done.2
  2.7 10.8 %shard_map.118 = f32[4,392,128]{2,1,0:T(8,128)S(1)} custom-call(s32[128,128]{1,0:T(8,128)S(1)} %bitcast.23, f32[8,128,128]{2,1,0:T(8,128)S(1)} %bitcast.20, f32[4,2,128]{2,1,0:T(2,128)S(1)} %bitcast.21), custom_call_target="tpu_custom_call" | custom-call | flops 1073741824 | bytes 2097152 | tf_op jit(solution)/shard_map/pallas_call | solution.py:200
  13.5 15.9 %all_to_all.15.message_ref = f32[4,392,128]{2,1,0:T(8,128)S(1)} all-to-all(f32[4,392,128]{2,1,0:T(8,128)S(1)} %shard_map.118), channel_id=1, replica_groups=mesh['tm'=4,'lev'=8] {'tm'}, dimensions={0} | all-to-all | bytes 1605632 | tf_op jit(solution)/shard_map/all_to_all | solution.py:520
  29.4 4.5 %all-to-all-start.1 = ((f32[4,256,512]{2,1,0:T(8,128)}), f32[4,256,512]{2,1,0:T(8,128)}, u32[]{:S(2)}, u32[]{:S(2)}) async-start(f32[4,256,512]{2,1,0:T(8,128)} %bitcast.3), calls=%async_computation.1 | async-start | bytes 4194304 | tf_op jit(solution)/shard_map/all_to_all | solution.py:525
  33.9 1.2 %constant_dynamic-slice_fusion.scale_ref = f32[2,128]{1,0:T(2,128)} fusion(f32[64,128]{1,0:T(8,128)} %param.16, s32[]{:T(128)S(6)} %dynamic_slice.10), kind=kLoop, calls=%fused_computation.4 | loop fusion | bytes 2052 | tf_op jit(solution)/shard_map/dynamic_slice | solution.py:533
  35.1 0.2 slice.14
  35.3 0.2 slice.15
  35.5 0.1 pad_maximum_fusion
  35.6 9.9 %shard_map.119.field_ref = f32[4,16,64,128]{3,2,1,0:T(8,128)S(1)} custom-call(s32[512]{0:T(512)S(1)} %bitcast.22, f32[4,392,128]{2,1,0:T(8,128)S(1)} %all_to_all.15.message_ref), custom_call_target="tpu_custom_call" | custom-call | flops 8589934592 | bytes 4194304 | tf_op jit(solution)/shard_map/pallas_call | solution.py:268
  45.4 0.0 copy-start.1
  45.5 1.3 %copy-done.1 = f32[4,16,64,128]{3,2,1,0:T(8,128)} copy-done((f32[4,16,64,128]{3,2,1,0:T(8,128)}, f32[4,16,64,128]{3,2,1,0:T(8,128)S(1)}, u32[]{:S(2)}) %copy-start.1) | copy-done | bytes 2097176
  46.8 12.8 %all-to-all-done.1.tangent_ref = f32[4,256,512]{2,1,0:T(8,128)} async-done(((f32[4,256,512]{2,1,0:T(8,128)}), f32[4,256,512]{2,1,0:T(8,128)}, u32[]{:S(2)}, u32[]{:S(2)}) %all-to-all-start.1) | async-done | bytes 2097184 | tf_op jit(solution)/shard_map/all_to_all | solution.py:525
  59.6 0.6 tile.11
  60.2 23.1 %shard_map.120 = f32[8,64,128]{2,1,0:T(8,128)} custom-call(f32[4,16,64,128]{3,2,1,0:T(8,128)} %copy-done.1, f32[4,256,512]{2,1,0:T(8,128)} %all-to-all-done.1.tangent_ref, f32[4,8,128]{2,1,0:T(8,128)} %bitcast.27, f32[2,128]{1,0:T(2,128)} %constant_dynamic-slice_fusion.scale_ref, bf16[256,512]{1,0:T(8,128)(2,1)} %constant.40.clone.fhigh_ref, ...), custom_call_target="tpu_custom_call" | custom-call | tf_op jit(solution)/shard_map/pallas_call | solution.py:472
  83.3 1.0 copy.14
  84.3 15.3 %all_to_all.16 = f32[32,16,128]{2,1,0:T(8,128)S(1)} all-to-all(f32[32,16,128]{2,1,0:T(8,128)S(1)} %bitcast.25), channel_id=1, replica_groups=mesh['tm'=4,'lev'=8] {'lev','tm'}, dimensions={0} | all-to-all | bytes 524288 | tf_op jit(solution)/shard_map/all_to_all | solution.py:541
  99.6 0.0 copy-done
  99.6 0.4 convolution_bitcast_fusion
  100.0 1.0 copy.15
  (4 shorter events, 0.1 us)
Async XLA Ops:
  0.0 99.6 %copy-start = (f32[64,64]{1,0:T(8,128)S(1)}, f32[64,64]{1,0:T(8,128)}, u32[]{:S(2)}) copy-start(f32[64,64]{1,0:T(8,128)} %param.17) | copy-start | bytes 49156
  1.9 0.8 copy-start.2
  29.4 30.2 %all-to-all-start.1 = ((f32[4,256,512]{2,1,0:T(8,128)}), f32[4,256,512]{2,1,0:T(8,128)}, u32[]{:S(2)}, u32[]{:S(2)}) async-start(f32[4,256,512]{2,1,0:T(8,128)} %bitcast.3), calls=%async_computation.1 | async-start | bytes 4194304 | tf_op jit(solution)/shard_map/all_to_all | solution.py:525
  45.4 1.3 %copy-start.1 = (f32[4,16,64,128]{3,2,1,0:T(8,128)}, f32[4,16,64,128]{3,2,1,0:T(8,128)S(1)}, u32[]{:S(2)}) copy-start(f32[4,16,64,128]{3,2,1,0:T(8,128)S(1)} %shard_map.119.field_ref) | copy-start | bytes 6291460

commit v3 on v2

--- a/solution.py
+++ b/solution.py
@@ -66,16 +66,60 @@
     return [np.asarray(a, np.float32) for a in (mu, diagonal, packed(up), packed(up * down))]
 
 
+def meet(axis):
+    count = lax.axis_size(axis)
+    me = lax.axis_index(axis)
+    barrier = pltpu.get_barrier_semaphore()
+    for d in range(1, count):
+        pl.semaphore_signal(
+            barrier, inc=1, device_id={axis: lax.rem(me + d, count)}, device_id_type=pl.DeviceIdType.MESH
+        )
+    pl.semaphore_wait(barrier, count - 1)
+
+
+def rates_for(tangent_ref, rows, section):
+    start = jnp.minimum(section * rows, tangent_ref.shape[0] - rows)
+    return tangent_ref.at[pl.ds(pl.multiple_of(start, SUBLANES), rows), :]
+
+
+def rate_copies(source, tangent_ref, place, sent, landed):
+    sections = lax.axis_size("tm")
+    copies = []
+    for d in range(1, sections):
+        peer = lax.rem(jnp.int32(source + d), sections)
+        copies.append(
+            pltpu.make_async_remote_copy(
+                src_ref=rates_for(tangent_ref, place.shape[0], peer),
+                dst_ref=place,
+                send_sem=sent.at[d],
+                recv_sem=landed,
+                device_id={"tm": peer},
+                device_id_type=pl.DeviceIdType.MESH,
+            )
+        )
+    return copies
+
+
 def bin_shape(lat_rows, lon_cols):
     tall = math.gcd(lat_rows, 32)
     return tall, (lat_rows // tall) * (lon_cols // LANES)
 
 
 def sort_kernel(
-    lon_cols, tall, bins, mine, cell_ref, innov_ref, damp_ref, out_ref, lane_from, sub_from, swaps,
+    lon_cols, tall, bins, mine, cell_ref, innov_ref, damp_ref, tangent_ref, out_ref, rate_ref,
+    lane_from, sub_from, swaps, sent, landed,
 ):
     levels, deep, _ = innov_ref.shape
     sections = out_ref.shape[0]
+    me = lax.axis_index("tm")
+    meet("tm")
+    copies = rate_copies(sections - 1, tangent_ref, rate_ref, sent, landed)
+
+    @pl.when(me == sections - 1)
+    def _():
+        for copy in copies:
+            copy.start()
+
     blocks = deep // SUBLANES
     low_bits, mid_bits, top_bits = (n.bit_length() - 1 for n in (blocks, SUBLANES, LANES))
     mid_end = low_bits + mid_bits
@@ -157,10 +201,13 @@
         below = sum(jnp.where(key < b * span, 1.0, 0.0) for key in keys)
         below = jnp.sum(jnp.sum(below, 0, keepdims=True), 1, keepdims=True)
         edges = jnp.where(lane[:1] == b, below, edges)
-    extra = damp_ref.shape[1]
+    extra = mine * damp_ref.shape[1] // LANES
+    first = lax.axis_index("lev") * levels
     base = (mine + 1) * deep
     for s in range(sections):
-        tail = [damp_ref[s], edges, jnp.zeros((SUBLANES - extra - 1, LANES), F32)]
+        place = jnp.minimum(first + s * mine, damp_ref.shape[0] - mine)
+        rows = [damp_ref[pl.ds(place + k, 1), :] for k in range(mine)]
+        tail = rows + [edges, jnp.zeros((SUBLANES - extra - 1, LANES), F32)]
         out_ref[s, base : base + SUBLANES, :] = jnp.concatenate(tail, 0)
         for k in range(mine):
             if s * mine + k >= levels:
@@ -188,10 +235,18 @@
 
     lax.fori_loop(0, levels, move, 0)
 
-
-def sorted_message(cells, innov, damp, mine, lat_rows, lon_cols):
+    @pl.when(me == sections - 1)
+    def _():
+        for copy in copies:
+            copy.wait_send()
+
+    @pl.when(me != sections - 1)
+    def _():
+        copies[0].wait_recv()
+
+
+def sorted_message(cells, innov, damp, tangent, sections, mine, lat_rows, lon_cols):
     levels, deep, _ = innov.shape
-    sections, extra, _ = damp.shape
     blocks = deep // SUBLANES
     low_bits, mid_bits, top_bits = (n.bit_length() - 1 for n in (blocks, SUBLANES, LANES))
     all_bits = low_bits + mid_bits + top_bits
@@ -199,27 +254,47 @@
     swap_count = sum(min(stage, low_bits) for stage in range(1, all_bits + 1))
     return pl.pallas_call(
         functools.partial(sort_kernel, lon_cols, tall, bins, mine),
-        in_specs=[pl.BlockSpec(memory_space=pltpu.VMEM)] * 3,
-        out_specs=pl.BlockSpec(memory_space=pltpu.VMEM),
-        out_shape=jax.ShapeDtypeStruct((sections, (mine + 1) * deep + SUBLANES, LANES), F32),
+        in_specs=[pl.BlockSpec(memory_space=pltpu.VMEM)] * 3 + [pl.BlockSpec(memory_space=pl.ANY)],
+        out_specs=[pl.BlockSpec(memory_space=pltpu.VMEM), pl.BlockSpec(memory_space=pl.ANY)],
+        out_shape=[
+            jax.ShapeDtypeStruct((sections, (mine + 1) * deep + SUBLANES, LANES), F32),
+            jax.ShapeDtypeStruct((mine * lat_rows, lon_cols), F32),
+        ],
         scratch_shapes=[
             pltpu.VMEM((top_bits, blocks, SUBLANES, LANES), jnp.int32),
             pltpu.VMEM((top_bits + mid_bits, blocks, SUBLANES, LANES), jnp.int32),
             pltpu.VMEM((swap_count, max(1, blocks // 2), SUBLANES, LANES), jnp.int32),
+            pltpu.SemaphoreType.DMA((sections,)),
+            pltpu.SemaphoreType.DMA,
         ],
-        compiler_params=pltpu.CompilerParams(vmem_limit_bytes=VMEM_BYTES // 2),
+        compiler_params=pltpu.CompilerParams(
+            collective_id=2, has_side_effects=True, vmem_limit_bytes=10 * 2**20
+        ),
         cost_estimate=pl.CostEstimate(flops=2**30, bytes_accessed=2**21, transcendentals=0),
-    )(cells, innov, damp)
-
-
-def forcing_kernel(mine, tall, edge_ref, message_ref, out_ref):
+    )(cells, innov, damp, tangent)
+
+
+def forcing_kernel(
+    mine, extra, tall, message_ref, tangent_ref, out_ref, rate_ref, run_ref, edge_ref, edge_sem, sent, landed,
+):
     times = message_ref.shape[0]
     bins = out_ref.shape[1]
+    me = lax.axis_index("tm")
+    meet("tm")
+    traffic = [rate_copies(t, tangent_ref, rate_ref.at[t - 1], sent, landed.at[t]) for t in range(1, times - 1)]
+    for t, copies in enumerate(traffic, 1):
+
+        @pl.when(me == t)
+        def _():
+            for copy in copies:
+                copy.start()
+
     deep = (message_ref.shape[1] - SUBLANES) // (mine + 1)
     chunks = deep // 2
     span = tall * LANES
-    stride = edge_ref.shape[0] // times
-    out_ref[...] = jnp.zeros_like(out_ref)
+    load = pltpu.make_async_copy(message_ref.at[:, (mine + 1) * deep + extra, :], edge_ref, edge_sem)
+    load.start()
+    run_ref[:, 0] = jnp.zeros(run_ref.shape[:1] + run_ref.shape[2:], F32)
     col_ids = lax.broadcasted_iota(jnp.int32, (LANES, 2 * LANES), 0).astype(F32).astype(BF16)
     row_ids = lax.broadcasted_iota(jnp.int32, (tall, 2 * LANES), 0).astype(F32).astype(BF16)
     one, none = jnp.ones((), BF16), jnp.zeros((), BF16)
@@ -240,53 +315,290 @@
 
     total = chunks + bins - 1
     unroll = 4
+    load.wait()
 
     def walk(s, state):
         fields, nexts = [], []
         for t in range(times):
-            b, c = state[t]
+            b, c, same = state[t]
             for u in range(unroll):
-                live = s * unroll + u < total
-                fields.append((t, b, visit(t, b, c, live)))
-                stay = edge_ref[t * stride + b + 1] > (c + 1) * 2 * LANES
-                b, c = (
-                    jnp.minimum(jnp.where(stay, b, b + 1), bins - 1),
-                    jnp.minimum(jnp.where(stay, c + 1, c), chunks - 1),
-                )
-            nexts.append((b, c))
-        for t, b, field in fields:
-            out_ref[t, b] += field
+                place = s * unroll + u
+                fields.append((t, place, same, visit(t, b, c, place < total)))
+                stay = (edge_ref[t, b + 1].astype(jnp.int32) > (c + 1) * 2 * LANES).astype(jnp.int32)
+                after = jnp.minimum(b + 1 - stay, bins - 1)
+                same = (after == b).astype(F32)
+                b, c = after, jnp.minimum(c + stay, chunks - 1)
+            nexts.append((b, c, same))
+        for t, place, same, field in fields:
+            run_ref[t, place + 1] = run_ref[t, place] * same + field
         return tuple(nexts)
 
     start = jnp.int32(0)
-    lax.fori_loop(0, -(-total // unroll), walk, tuple((start, start) for _ in range(times)))
-
-
-def forcing_fields(message, edges, mine, lat_rows, lon_cols):
+    steps = -(-total // unroll)
+    lax.fori_loop(0, steps, walk, tuple((start, start, jnp.float32(0)) for _ in range(times)))
+
+    def place_bin(b, carry):
+        for t in range(times):
+            end = edge_ref[t, b + 1].astype(jnp.int32)
+            last = b + jnp.maximum((end + 2 * LANES - 1) // (2 * LANES) - 1, 0)
+            last = jnp.where(b == bins - 1, steps * unroll - 1, last)
+            last = jnp.minimum(jnp.maximum(last, 0), steps * unroll - 1)
+            out_ref[t, b] = run_ref[t, last + 1]
+        return carry
+
+    lax.fori_loop(0, bins, place_bin, 0)
+    for t, copies in enumerate(traffic, 1):
+
+        @pl.when(me == t)
+        def _():
+            for copy in copies:
+                copy.wait_send()
+
+        @pl.when(me != t)
+        def _():
+            copies[0].wait_recv()
+
+
+def forcing_fields(message, tangent, mine, extra, lat_rows, lon_cols):
     times = message.shape[0]
     tall, bins = bin_shape(lat_rows, lon_cols)
+    deep = (message.shape[1] - SUBLANES) // (mine + 1)
+    places = -(-(deep // 2 + bins - 1) // 4) * 4 + 1
     return pl.pallas_call(
-        functools.partial(forcing_kernel, mine, tall),
-        in_specs=[pl.BlockSpec(memory_space=pltpu.SMEM), pl.BlockSpec(memory_space=pltpu.VMEM)],
-        out_specs=pl.BlockSpec(memory_space=pltpu.VMEM),
-        out_shape=jax.ShapeDtypeStruct((times, bins, mine * tall, LANES), F32),
-        compiler_params=pltpu.CompilerParams(vmem_limit_bytes=VMEM_BYTES // 2),
+        functools.partial(forcing_kernel, mine, extra, tall),
+        in_specs=[pl.BlockSpec(memory_space=pltpu.VMEM), pl.BlockSpec(memory_space=pl.ANY)],
+        out_specs=[pl.BlockSpec(memory_space=pltpu.VMEM), pl.BlockSpec(memory_space=pl.ANY)],
+        out_shape=[
+            jax.ShapeDtypeStruct((times, bins, mine * tall, LANES), F32),
+            jax.ShapeDtypeStruct((times - 2, mine * lat_rows, lon_cols), F32),
+        ],
+        scratch_shapes=[
+            pltpu.VMEM((times, places, mine * tall, LANES), F32),
+            pltpu.SMEM((times, LANES), F32),
+            pltpu.SemaphoreType.DMA,
+            pltpu.SemaphoreType.DMA((times,)),
+            pltpu.SemaphoreType.DMA((times,)),
+        ],
+        compiler_params=pltpu.CompilerParams(
+            collective_id=3, has_side_effects=True, vmem_limit_bytes=4 * times * places * mine * tall * LANES + 10 * 2**20
+        ),
         cost_estimate=pl.CostEstimate(flops=2**33, bytes_accessed=2**22, transcendentals=0),
-    )(edges, message)
+    )(message, tangent)
 
 
 def lanes_at(value, index):
     return jnp.take_along_axis(value, jnp.broadcast_to(index, value.shape), axis=1, mode="promise_in_bounds")
 
 
+def legendre_tables(half, mu_ref, diag_ref, up_ref, both_ref, high, low, left, right):
+    groups, width = mu_ref.shape
+    waves = high.shape[1]
+    pack = width // half
+    deep = LANES // pack
+    lane = lax.broadcasted_iota(jnp.int32, (1, LANES), 1)
+    sub = lax.broadcasted_iota(jnp.int32, (groups, width), 0)
+    orders = sub * pack + lax.broadcasted_iota(jnp.int32, (groups, width), 1) // half
+
+    def advance(n, state):
+        one, two = state
+        place = pl.ds(pl.multiple_of(n // deep * groups, groups), groups)
+        base = (n % deep) * pack
+
+        def spread_out(ref):
+            value = ref[place, :]
+            return jnp.concatenate([lanes_at(value, base + lane // half + i * (LANES // half)) for i in range(width // LANES)], 1)
+
+        recurred = spread_out(up_ref) * (mu_ref[...] * one) - spread_out(both_ref) * two
+        value = jnp.where(orders == n, diag_ref[...], recurred)
+        row = (n % 2) * (waves // 2) + n // 2
+        left[pl.ds(row, groups, stride=waves), :] = value[:, :LANES]
+        right[pl.ds(row, groups, stride=waves), :] = value[:, LANES:]
+        return value, one
+
+    zero = 0.0 * mu_ref[...]
+    lax.fori_loop(0, waves, advance, (zero, zero), unroll=8)
+
+    def split(g, carry):
+        for i, ref in enumerate((left, right)):
+            upper, lower = halves(ref[pl.ds(pl.multiple_of(g * waves, waves), waves), :])
+            high[g, :, i * LANES : (i + 1) * LANES] = upper
+            low[g, :, i * LANES : (i + 1) * LANES] = lower
+        return carry
+
+    lax.fori_loop(0, groups, split, 0, unroll=4)
+
+
+def exchange_kernel(
+    half, message_ref, mu_ref, diag_ref, up_ref, both_ref, out_ref, high_ref, low_ref,
+    high, low, left, right, sent, landed, own, stored,
+):
+    sections = lax.axis_size("tm")
+    me = lax.axis_index("tm")
+    meet("tm")
+    copies = []
+    for d in range(1, sections):
+        peer = lax.rem(me + d, sections)
+        copies.append(
+            pltpu.make_async_remote_copy(
+                src_ref=message_ref.at[peer],
+                dst_ref=out_ref.at[me],
+                send_sem=sent.at[d],
+                recv_sem=landed.at[d],
+                device_id={"tm": peer},
+                device_id_type=pl.DeviceIdType.MESH,
+            )
+        )
+        copies[-1].start()
+    keep = pltpu.make_async_copy(message_ref.at[me], out_ref.at[me], own)
+    keep.start()
+    legendre_tables(half, mu_ref, diag_ref, up_ref, both_ref, high, low, left, right)
+    saves = [
+        pltpu.make_async_copy(high, high_ref, stored.at[0]),
+        pltpu.make_async_copy(low, low_ref, stored.at[1]),
+    ]
+    for save in saves:
+        save.start()
+    keep.wait()
+    for save in saves:
+        save.wait()
+    for copy in copies:
+        copy.wait()
+
+
+def exchanged(message, lat_rows, waves):
+    mu, diagonal, up, both = legendre_coefficients(lat_rows, waves)
+    groups, width = mu.shape
+    sections = message.shape[0]
+    table = jax.ShapeDtypeStruct((groups, waves, width), BF16)
+    vmem = pl.BlockSpec(memory_space=pltpu.VMEM)
+    return pl.pallas_call(
+        functools.partial(exchange_kernel, lat_rows // 2),
+        in_specs=[vmem] * 5,
+        out_specs=[vmem, pl.BlockSpec(memory_space=pl.ANY), pl.BlockSpec(memory_space=pl.ANY)],
+        out_shape=[jax.ShapeDtypeStruct(message.shape, F32), table, table],
+        scratch_shapes=[
+            pltpu.VMEM((groups, waves, width), BF16),
+            pltpu.VMEM((groups, waves, width), BF16),
+            pltpu.VMEM((waves * groups, LANES), F32),
+            pltpu.VMEM((waves * groups, LANES), F32),
+            pltpu.SemaphoreType.DMA((sections,)),
+            pltpu.SemaphoreType.DMA((sections,)),
+            pltpu.SemaphoreType.DMA,
+            pltpu.SemaphoreType.DMA((2,)),
+        ],
+        compiler_params=pltpu.CompilerParams(
+            collective_id=0, has_side_effects=True, vmem_limit_bytes=16 * 2**20
+        ),
+        cost_estimate=pl.CostEstimate(flops=2**32, bytes_accessed=2**23, transcendentals=0),
+    )(message, mu, diagonal, up, both)
+
+
+def gather_kernel(total_ref, out_ref, sent, landed, own):
+    sections, groups = lax.axis_size("tm"), lax.axis_size("lev")
+    count = sections * groups
+    me = lax.axis_index("lev") * sections + lax.axis_index("tm")
+
+    def place(index):
+        return {"tm": lax.rem(index, sections), "lev": lax.div(index, sections)}
+
+    barrier = pltpu.get_barrier_semaphore()
+
+    def greet(d, carry):
+        pl.semaphore_signal(
+            barrier, inc=1, device_id=place(lax.rem(me + d, count)), device_id_type=pl.DeviceIdType.MESH
+        )
+        return carry
+
+    lax.fori_loop(1, count, greet, 0)
+    keep = pltpu.make_async_copy(total_ref.at[me], out_ref.at[me], own)
+    keep.start()
+    pl.semaphore_wait(barrier, count - 1)
+
+    def copy_to(d):
+        peer = lax.rem(me + d, count)
+        return pltpu.make_async_remote_copy(
+            src_ref=total_ref.at[peer],
+            dst_ref=out_ref.at[me],
+            send_sem=sent.at[d],
+            recv_sem=landed.at[d],
+            device_id=place(peer),
+            device_id_type=pl.DeviceIdType.MESH,
+        )
+
+    def send(d, carry):
+        copy_to(d).start()
+        return carry
+
+    def finish(d, carry):
+        copy_to(d).wait()
+        return carry
+
+    lax.fori_loop(1, count, send, 0)
+    keep.wait()
+    lax.fori_loop(1, count, finish, 0)
+
+
+def gathered(total):
+    count = total.shape[0]
+    vmem = pl.BlockSpec(memory_space=pltpu.VMEM)
+    return pl.pallas_call(
+        gather_kernel,
+        in_specs=[vmem],
+        out_specs=vmem,
+        out_shape=jax.ShapeDtypeStruct(total.shape, F32),
+        scratch_shapes=[
+            pltpu.SemaphoreType.DMA((count,)),
+            pltpu.SemaphoreType.DMA((count,)),
+            pltpu.SemaphoreType.DMA,
+        ],
+        compiler_params=pltpu.CompilerParams(collective_id=1, has_side_effects=True, vmem_limit_bytes=4 * 2**20),
+        cost_estimate=pl.CostEstimate(flops=2**30, bytes_accessed=2**20, transcendentals=0),
+    )(total)
+
+
 def sweep_kernel(
-    sections, field_ref, tangent_ref, damp_ref, scale_ref, fhigh_ref, flow_ref, mu_ref, diag_ref, up_ref, both_ref,
-    out_ref, left, right, high, low, even, odd, packed, total, adjoint, order,
+    base, field_hbm, own_hbm, rate_hbm, later_hbm, message_hbm, spread_ref, fhigh_ref, flow_ref, high_hbm, low_hbm,
+    out_ref, field_ref, tangent_ref, tail_ref, high, low, even, odd, packed, total, adjoint, order,
+    field_sem, tangent_sem, tail_sem, table_sem,
 ):
     times, rows, lon_cols = tangent_ref.shape
+    sections = lax.axis_size("tm")
+    load_tail = pltpu.make_async_copy(message_hbm.at[:, pl.ds(base, SUBLANES), :], tail_ref, tail_sem)
+    load_tables = [
+        pltpu.make_async_copy(high_hbm, high, table_sem.at[0]),
+        pltpu.make_async_copy(low_hbm, low, table_sem.at[1]),
+    ]
+
+    def load_field(t):
+        return pltpu.make_async_copy(field_hbm.at[t], field_ref.at[t], field_sem.at[t])
+
+    me = lax.axis_index("tm")
+    own = rates_for(own_hbm, rows, me)
+
+    def load_tangent(t):
+        return pltpu.make_async_copy(own, tangent_ref.at[t], tangent_sem.at[t])
+
+    def start_tangent(t):
+        @pl.when(me == t)
+        def _():
+            load_tangent(t).start()
+
+        @pl.when(me != t)
+        def _():
+            source = rate_hbm if t == times - 1 else later_hbm.at[t - 1]
+            pltpu.make_async_copy(source, tangent_ref.at[t], tangent_sem.at[t]).start()
+
+    load_field(times - 1).start()
+    load_tail.start()
+    for load in load_tables:
+        load.start()
+    start_tangent(times - 1)
+    for t in range(times - 2, -1, -1):
+        load_field(t).start()
+        if t > 0:
+            start_tangent(t)
     bins = field_ref.shape[1]
-    groups, width = mu_ref.shape
-    waves = high.shape[1]
+    groups, waves, width = high.shape
     lat_rows = width * groups * 2 // waves
     half = lat_rows // 2
     pack = width // half
@@ -294,43 +606,12 @@
     levels = rows // lat_rows
     tall = field_ref.shape[2] // levels
     across = lon_cols // LANES
-    group = damp_ref.shape[1]
+    group = 4 * levels
     mid = group // 2
 
     lane = lax.broadcasted_iota(jnp.int32, (1, LANES), 1)
     in_first = lane < half
     fold = lane % half
-    sub = lax.broadcasted_iota(jnp.int32, (groups, width), 0)
-    orders = sub * pack + lax.broadcasted_iota(jnp.int32, (groups, width), 1) // half
-
-    def advance(n, state):
-        one, two = state
-        place = pl.ds(pl.multiple_of(n // deep * groups, groups), groups)
-        base = (n % deep) * pack
-
-        def spread_out(ref):
-            value = ref[place, :]
-            return jnp.concatenate([lanes_at(value, base + lane // half + i * (LANES // half)) for i in range(width // LANES)], 1)
-
-        recurred = spread_out(up_ref) * (mu_ref[...] * one) - spread_out(both_ref) * two
-        value = jnp.where(orders == n, diag_ref[...], recurred)
-        row = (n % 2) * (waves // 2) + n // 2
-        left[pl.ds(row, groups, stride=waves), :] = value[:, :LANES]
-        right[pl.ds(row, groups, stride=waves), :] = value[:, LANES:]
-        return value, one
-
-    zero = 0.0 * mu_ref[...]
-    lax.fori_loop(0, waves, advance, (zero, zero), unroll=8)
-
-    def split(g, carry):
-        for i, ref in enumerate((left, right)):
-            upper, lower = halves(ref[pl.ds(pl.multiple_of(g * waves, waves), waves), :])
-            high[g, :, i * LANES : (i + 1) * LANES] = upper
-            low[g, :, i * LANES : (i + 1) * LANES] = lower
-        return carry
-
-    lax.fori_loop(0, groups, split, 0, unroll=4)
-
     in_high = lax.broadcasted_iota(jnp.int32, (group, LANES), 0) < mid
     n_even = lax.broadcasted_iota(jnp.int32, (group, LANES), 1) < waves // 2
     lat_south = lax.broadcasted_iota(jnp.int32, (group, LANES), 1) < half
@@ -340,7 +621,18 @@
         lax.broadcasted_iota(jnp.int32, (waves, LANES), 0) % (LANES // half)
     )
 
+    load_tail.wait()
+
+    def damp_of(t):
+        index = 2 * (lane % (waves // 2)) + lane // (waves // 2)
+        row = lax.broadcasted_iota(jnp.int32, (group, LANES), 0) % mid // 2
+        value = jnp.zeros((group, LANES), F32)
+        for k in range(levels):
+            value = jnp.where(row == k, jnp.broadcast_to(tail_ref[t, k : k + 1, :], value.shape), value)
+        return lanes_at(value, index)
+
     def analyse(t):
+        load_field(t).wait()
         field = [
             jnp.concatenate([field_ref[t, h + i, k * tall : (k + 1) * tall, :] for i in range(across)], 1)
             for k in range(levels)
@@ -409,7 +701,12 @@
     def step(s, carry):
         t = times - 1 - s
         analyse(t)
-        damp = damp_ref[t]
+        damp = damp_of(t)
+
+        @pl.when(s == 0)
+        def _():
+            for load in load_tables:
+                load.wait()
 
         def wave(g, inner):
             for i, value in enumerate(spectral_of(g)):
@@ -431,6 +728,7 @@
         )
         upper, lower = halves(synth)
         gridded = dot(upper, fhigh_ref[...], NN) + dot(lower, fhigh_ref[...], NN) + dot(upper, flow_ref[...], NN)
+        load_tangent(t).wait()
         adjoint[...] = tangent_ref[t] * adjoint[...] + gridded
         return carry
 
@@ -447,36 +745,44 @@
     side = LANES // block_n
     deal = 2 * waves // side
     natural = (lane % 2) * (waves // 2) + lane // 2
+    lev_dev = spread_ref.shape[0] // lax.axis_size("lev")
+    first = lax.axis_index("lev") * lev_dev + lax.axis_index("tm") * levels
+    first = jnp.minimum(first, spread_ref.shape[0] - levels)
     for k in range(levels):
         for p in range(2):
             value = total[pl.ds(2 * k + p, waves, stride=group), :]
-            order[pl.ds(p, waves, stride=2), :] = lanes_at(value, natural) * scale_ref[k : k + 1, :]
+            order[pl.ds(p, waves, stride=2), :] = lanes_at(value, natural) * spread_ref[pl.ds(first + k, 1), :]
         blocks = [order[pl.ds(q, deal, stride=side), :] for q in range(side)]
         for s in range(sections):
             value = blocks[0] if s == 0 else pltpu.roll(blocks[0], (-s * block_n) % LANES, 1)
             for q in range(1, side):
                 moved = blocks[q] if q == s else pltpu.roll(blocks[q], ((q - s) * block_n) % LANES, 1)
                 value = jnp.where(lane // block_n == q, moved, value)
-            out_ref[s * levels + k] = value
-
-
-def sweep(fields, tangent, damp, scale, lat_rows, waves, sections):
-    times, rows, lon_cols = tangent.shape
-    group = damp.shape[1]
+            rows = deal * sections // out_ref.shape[0]
+            for b in range(out_ref.shape[0] // sections):
+                out_ref[b * sections + s, k * rows : (k + 1) * rows, :] = value[b * rows : (b + 1) * rows]
+
+
+def sweep(fields, tangent, rate, later, message, spread, high, low, lat_rows, base, sections, blocks):
+    times = fields.shape[0]
+    rows, lon_cols = rate.shape
     levels = rows // lat_rows
+    group = 4 * levels
+    groups, waves, width = high.shape
     fourier = fourier_rows(lon_cols, waves)
     fhigh = fourier.astype(jnp.bfloat16)
     flow = (fourier - fhigh.astype(np.float32)).astype(jnp.bfloat16)
-    mu, diagonal, up, both = legendre_coefficients(lat_rows, waves)
-    groups, width = mu.shape
+    deal = 2 * waves * (waves // sections) // LANES // blocks
+    vmem, hbm = pl.BlockSpec(memory_space=pltpu.VMEM), pl.BlockSpec(memory_space=pl.ANY)
     return pl.pallas_call(
-        functools.partial(sweep_kernel, sections),
-        in_specs=[pl.BlockSpec(memory_space=pltpu.VMEM)] * 10,
-        out_specs=pl.BlockSpec(memory_space=pltpu.VMEM),
-        out_shape=jax.ShapeDtypeStruct((sections * levels, 2 * waves * (waves // sections) // LANES, LANES), F32),
+        functools.partial(sweep_kernel, base),
+        in_specs=[hbm, hbm, hbm, hbm, hbm, vmem, vmem, vmem, hbm, hbm],
+        out_specs=vmem,
+        out_shape=jax.ShapeDtypeStruct((blocks * sections, levels * deal, LANES), F32),
         scratch_shapes=[
-            pltpu.VMEM((waves * groups, LANES), F32),
-            pltpu.VMEM((waves * groups, LANES), F32),
+            pltpu.VMEM(fields.shape, F32),
+            pltpu.VMEM((times, rows, lon_cols), F32),
+            pltpu.VMEM((times, SUBLANES, LANES), F32),
             pltpu.VMEM((groups, waves, width), BF16),
             pltpu.VMEM((groups, waves, width), BF16),
             pltpu.VMEM((waves * group, LANES), F32),
@@ -485,16 +791,19 @@
             pltpu.VMEM((waves * group, LANES), F32),
             pltpu.VMEM((rows, lon_cols), F32),
             pltpu.VMEM((2 * waves, LANES), F32),
+            pltpu.SemaphoreType.DMA((times,)),
+            pltpu.SemaphoreType.DMA((times,)),
+            pltpu.SemaphoreType.DMA,
+            pltpu.SemaphoreType.DMA((2,)),
         ],
-        compiler_params=pltpu.CompilerParams(vmem_limit_bytes=VMEM_BYTES),
-    )(fields, tangent, damp, scale, fhigh, flow, mu, diagonal, up, both)
+        compiler_params=pltpu.CompilerParams(vmem_limit_bytes=24 * 2**20),
+        cost_estimate=pl.CostEstimate(flops=2**34, bytes_accessed=2**22, transcendentals=0),
+    )(fields, tangent, rate, later, message, spread, fhigh, flow, high, low)
 
 
 def shards(obs_cell, innovation, tangent, damping, spread, vertical):
     sections = lax.axis_size("tm")
     groups = lax.axis_size("lev")
-    me_tm = lax.axis_index("tm")
-    me_lev = lax.axis_index("lev")
     lev_dev, lat_rows, lon_cols = tangent.shape[1:]
     levels, waves = damping.shape[1:]
     mine = -(-lev_dev // sections)
@@ -508,38 +817,26 @@
 
     count = obs_cell.shape[1]
     deep = count // LANES
-    damp_block = pad_levels(lax.dynamic_slice_in_dim(damping[0], me_lev * lev_dev, lev_dev, 0), 0)
-    message = sorted_message(
+    message, rate = sorted_message(
         obs_cell.reshape(deep, LANES),
         innovation.reshape(lev_dev, deep, LANES),
-        damp_block.reshape(sections, mine * waves // LANES, LANES),
+        damping[0],
+        tangent.reshape(lev_dev * lat_rows, lon_cols),
+        sections,
         mine,
         lat_rows,
         lon_cols,
     )
-    message = lax.all_to_all(message, "tm", split_axis=0, concat_axis=0, tiled=True)
+    message, high, low = exchanged(message, lat_rows, waves)
     base = (mine + 1) * deep
-    extra = mine * waves // LANES
-    damp_mine = message[:, base : base + extra].reshape(sections, mine, waves)
-    edges = message[:, base + extra].astype(jnp.int32).reshape(sections * LANES)
-    rates = lax.all_to_all(
-        pad_levels(tangent[0], 0).reshape(sections, mine * lat_rows, lon_cols),
-        "tm", split_axis=0, concat_axis=0, tiled=True,
-    )
-    fields = forcing_fields(message, edges, mine, lat_rows, lon_cols)
-    damp_mine = jnp.concatenate([damp_mine[..., 0::2], damp_mine[..., 1::2]], -1)
-    damp_rows = jnp.tile(jnp.repeat(damp_mine, 2, axis=1), (1, 2, 1))
-    scale = pad_levels(lax.dynamic_slice_in_dim(spread, me_lev * lev_dev, lev_dev, 0), 0)
-    scale = lax.dynamic_slice_in_dim(scale, me_tm * mine, mine, 0)
-    total = sweep(fields, rates, damp_rows, scale, lat_rows, waves, sections)
+    rates = tangent.reshape(lev_dev * lat_rows, lon_cols)
+    fields, later = forcing_fields(message, rates, mine, mine * waves // LANES, lat_rows, lon_cols)
+    total = sweep(fields, rates, rate, later, message, spread, high, low, lat_rows, base, sections, groups)
 
     block_m = waves // groups
     block_n = waves // sections
-    deal = total.shape[1] // groups
-    outgoing = total.reshape(sections, mine, groups, deal, LANES)
-    outgoing = outgoing.transpose(2, 0, 1, 3, 4).reshape(groups * sections, mine * deal, LANES)
-    arrived = lax.all_to_all(outgoing, ("lev", "tm"), split_axis=0, concat_axis=0, tiled=True)
-    arrived = arrived.reshape(groups, padded, deal * LANES)[:, :lev_dev].reshape(levels, deal * LANES)
+    deal = total.shape[1] // mine
+    arrived = gathered(total).reshape(groups, padded, deal * LANES)[:, :lev_dev].reshape(levels, deal * LANES)
     result = jnp.einsum("kj,kx->jx", vertical, arrived, precision=PRECISE)
     return result.reshape(levels, block_m, 2, block_n)
 

time: 101 us -> 72.6 us (0.72)
  blocking collectives: 31.1 us -> 0 us
  Pallas kernels: 43.9 us -> 66.2 us
  waiting for transfers between devices: 12.8 us -> 0 us
  starting transfers between devices: 4.45 us -> 0 us
  local copies, waits for them, and re-layouts: 8.18 us -> 5.42 us
    all_to_all x2 -> x0, blocking collectives: 31.1 us -> none  [the longest x1 15.9 us: shards(): lax.all_to_all(message, 'tm', split_axis=0, concat_axis=0, tiled=True)]
    pallas_call x2 -> x4, Pallas kernels: 33 us -> 52.3 us  [the longest x1 14.5 us: gathered(): pl.pallas_call(gather_kernel, in_specs=[vmem], out_specs=vmem, out_shape=...]
    all_to_all x1 -> x0, waiting for transfers between devices: 12.8 us -> none  [shards(): lax.all_to_all(pad_levels(tangent[0], 0).reshape(sections, mine * lat_row...]
    all_to_all x1 -> x0, starting transfers between devices: 4.45 us -> none  [shards(): lax.all_to_all(pad_levels(tangent[0], 0).reshape(sections, mine * lat_row...]
    pallas_call x1, Pallas kernels: 10.8 us -> 14 us  [sorted_message(): pl.pallas_call(functools.partial(sort_kernel, lon_cols, tall, bins, mine)...]
    dynamic_slice x2 -> x0, local copies, waits for them, and re-layouts: 1.94 us -> none  [the longest x1 1.25 us: shards(): scale = lax.dynamic_slice_in_dim(scale, me_tm * mine, mine, 0)]
    unnamed x7 -> x25, local copies, waits for them, and re-layouts: 3.29 us -> 4.38 us
  transfers between devices with their start and end apart: 1 -> 0, of which waited for: 1 -> 0; matrix products, arithmetic and copies ran while one was open for 2% -> 0% of each run, Pallas kernels for 10% -> 0%
where the time goes in v3:
time: 72.6 us; the launch traced here: 72.2 us
  Pallas kernels  66.2 us (91%)
  local copies, waits for them, and re-layouts  5.42 us (7%)
    pallas_call x1, Pallas kernels, gathered(): pl.pallas_call(gather_kernel, in_specs=[vmem], out_specs=vmem, out_shape=...  14.5 us
    pallas_call x1, Pallas kernels, sweep(): pl.pallas_call(functools.partial(sweep_kernel, base), in_specs=[hbm, hbm,...  14.5 us
    pallas_call x1, Pallas kernels, sorted_message(): pl.pallas_call(functools.partial(sort_kernel, lon_cols, tall, bins, mine)...  14 us
    pallas_call x1, Pallas kernels, forcing_fields(): pl.pallas_call(functools.partial(forcing_kernel, mine, extra, tall), in_s...  12.6 us
    pallas_call x1, Pallas kernels, exchanged(): pl.pallas_call(functools.partial(exchange_kernel, lat_rows // 2), in_spec...  10.7 us
    unnamed x25, local copies, waits for them, and re-layouts  4.38 us

profile of v3, /device:TPU:0, one launch (start us, length us, event | category | flops | bytes accessed | tf_op | source)
XLA Modules:
  0.0 72.2 jit_solution(15592140345412070584)
XLA Ops:
  0.0 0.0 copy-start
  0.0 1.2 %copy.17 = f32[1,8,128,128]{3,2,1,0:T(8,128)S(1)} copy(f32[1,8,128,128]{3,1,2,0:T(8,128)} %bitcast.19) | data formatting | bytes 1048576
  1.2 0.0 copy-start.1
  1.2 1.6 %copy-done.1 = f32[1,8,128,512]{3,2,1,0:T(8,128)S(1)} copy-done((f32[1,8,128,512]{3,2,1,0:T(8,128)S(1)}, f32[1,8,128,512]{3,2,1,0:T(8,128)}, u32[]{:S(2)}) %copy-start.1) | copy-done | bytes 2097176
  2.8 0.0 copy-start.3
  2.8 0.8 %copy-done.3 = s32[1,16384]{1,0:T(1,128)S(1)} copy-done((s32[1,16384]{1,0:T(1,128)S(1)}, s32[1,16384]{1,0:T(1,128)}, u32[]{:S(2)}) %copy-start.3) | copy-done | bytes 65560
  3.6 0.0 copy-start.4
  3.6 0.8 %copy-done.4 = f32[1,64,128]{2,1,0:T(8,128)S(1)} copy-done((f32[1,64,128]{2,1,0:T(8,128)S(1)}, f32[1,64,128]{2,1,0:T(8,128)}, u32[]{:S(2)}) %copy-start.4) | copy-done | bytes 32792
  4.3 0.0 copy-start.8
  4.4 0.0 copy-start.9
  4.4 0.0 copy-start.10
  4.4 0.0 copy-start.11
  4.4 14.0 %shard_map.118 = (f32[4,392,128]{2,1,0:T(8,128)S(1)}, f32[256,512]{1,0:T(8,128)S(1)}) custom-call(s32[128,128]{1,0:T(8,128)S(1)} %bitcast.17, f32[8,128,128]{2,1,0:T(8,128)S(1)} %bitcast.13, f32[64,128]{1,0:T(8,128)S(1)} %bitcast.18, f32[1024,512]{1,0:T(8,128)S(1)} %bitcast.14), custom_call_target="tpu_custom_call" | custom-call | flops 1073741824 | bytes 2097152 | tf_op jit(solution)/shard_map/pallas_call | solution.py:255
  18.3 0.0 copy-done.8
  18.3 0.0 copy-done.9
  18.3 0.0 copy-done.10
  18.3 0.0 copy-done.11
  18.4 0.0 copy-start.2
  18.4 10.7 %shard_map.119 = (f32[4,392,128]{2,1,0:T(8,128)S(1)}, bf16[32,128,256]{2,1,0:T(8,128)(2,1)S(1)}, bf16[32,128,256]{2,1,0:T(8,128)(2,1)S(1)}) custom-call(f32[4,392,128]{2,1,0:T(8,128)S(1)} %get-tuple-element.12.message_ref, f32[32,256]{1,0:T(8,128)S(1)} %copy-done.11, f32[32,256]{1,0:T(8,128)S(1)} %copy-done.10, f32[128,128]{1,0:T(8,128)S(1)} %copy-done.9, ...), custom_call_target="tpu_custom_call" | custom-call | flops 4294967296 | bytes 8388608 | tf_op jit(solution)/shard_map/pallas_call | solution.py:474
  29.1 0.0 copy-done.2
  29.1 0.0 copy-start.5
  29.1 0.0 copy-start.6
  29.1 0.0 copy-start.7
  29.1 12.6 %shard_map.120 = (f32[4,16,64,128]{3,2,1,0:T(8,128)S(1)}, f32[2,256,512]{2,1,0:T(8,128)S(1)}) custom-call(f32[4,392,128]{2,1,0:T(8,128)S(1)} %get-tuple-element.13.message_ref.message_hbm, f32[1024,512]{1,0:T(8,128)S(1)} %bitcast.15), custom_call_target="tpu_custom_call" | custom-call | flops 8589934592 | bytes 4194304 | tf_op jit(solution)/shard_map/pallas_call | solution.py:367
  41.8 0.0 copy-done.5
  41.8 0.0 copy-done.6
  41.8 0.0 copy-done.7
  41.8 14.5 %shard_map.121.total_ref = f32[32,16,128]{2,1,0:T(8,128)S(1)} custom-call(f32[4,16,64,128]{3,2,1,0:T(8,128)S(1)} %get-tuple-element.14.field_hbm, f32[1024,512]{1,0:T(8,128)S(1)} %bitcast.16, f32[256,512]{1,0:T(8,128)S(1)} %get-tuple-element.15.rate_hbm, f32[2,256,512]{2,1,0:T(8,128)S(1)} %get-tuple-element.16.later_hbm, ...), custom_call_target="tpu_custom_call" | custom-call | flops 17179869184 | bytes 4194304 | tf_op jit(solution)/shard_map/pallas_call | solution.py:777
  56.3 14.5 %shard_map.122 = f32[32,16,128]{2,1,0:T(8,128)S(1)} custom-call(f32[32,16,128]{2,1,0:T(8,128)S(1)} %shard_map.121.total_ref), custom_call_target="tpu_custom_call" | custom-call | flops 1073741824 | bytes 1048576 | tf_op jit(solution)/shard_map/pallas_call | solution.py:544
  70.8 0.0 copy-done
  70.8 0.4 convolution_bitcast_fusion
  71.2 1.0 %copy.14 = f32[64,1024]{0,1:T(8,128)} copy(f32[64,1024]{1,0:T(8,128)S(1)} %convolution_bitcast_fusion) | data formatting | bytes 524288 | tf_op jit(solution)/shard_map/kj,kx->jx/dot_general | solution.py:840
  (1 shorter events, 0.0 us)
Async XLA Ops:
  0.0 70.8 %copy-start = (f32[64,64]{1,0:T(8,128)S(1)}, f32[64,64]{1,0:T(8,128)}, u32[]{:S(2)}) copy-start(f32[64,64]{1,0:T(8,128)} %param.17) | copy-start | bytes 49156
  1.2 1.6 %copy-start.1 = (f32[1,8,128,512]{3,2,1,0:T(8,128)S(1)}, f32[1,8,128,512]{3,2,1,0:T(8,128)}, u32[]{:S(2)}) copy-start(f32[1,8,128,512]{3,2,1,0:T(8,128)} %param.14) | copy-start | bytes 6291460
  2.8 0.8 %copy-start.3 = (s32[1,16384]{1,0:T(1,128)S(1)}, s32[1,16384]{1,0:T(1,128)}, u32[]{:S(2)}) copy-start(s32[1,16384]{1,0:T(1,128)} %param.12) | copy-start | bytes 196612
  3.6 0.8 %copy-start.4 = (f32[1,64,128]{2,1,0:T(8,128)S(1)}, f32[1,64,128]{2,1,0:T(8,128)}, u32[]{:S(2)}) copy-start(f32[1,64,128]{2,1,0:T(8,128)} %param.15) | copy-start | bytes 98308
  4.3 14.0 %copy-start.8 = (f32[128,128]{1,0:T(8,128)S(1)}, f32[128,128]{1,0:T(8,128)}, u32[]{:S(2)}) copy-start(f32[128,128]{1,0:T(8,128)} %constant.15.clone.both_ref) | copy-start | bytes 196612
  4.4 14.0 %copy-start.9 = (f32[128,128]{1,0:T(8,128)S(1)}, f32[128,128]{1,0:T(8,128)}, u32[]{:S(2)}) copy-start(f32[128,128]{1,0:T(8,128)} %constant.14.clone.up_ref) | copy-start | bytes 196612
  4.4 14.0 %copy-start.10 = (f32[32,256]{1,0:T(8,128)S(1)}, f32[32,256]{1,0:T(8,128)}, u32[]{:S(2)}) copy-start(f32[32,256]{1,0:T(8,128)} %constant.13.clone.diag_ref) | copy-start | bytes 98308
  4.4 14.0 %copy-start.11 = (f32[32,256]{1,0:T(8,128)S(1)}, f32[32,256]{1,0:T(8,128)}, u32[]{:S(2)}) copy-start(f32[32,256]{1,0:T(8,128)} %constant.12.clone.mu_ref) | copy-start | bytes 98308
  18.4 10.7 %copy-start.2 = (f32[1,8,128,512]{3,2,1,0:T(8,128)S(1)}, f32[1,8,128,512]{3,2,1,0:T(8,128)}, u32[]{:S(2)}) copy-start(f32[1,8,128,512]{3,2,1,0:T(8,128)} %param.14) | copy-start | bytes 6291460
  29.1 12.7 %copy-start.5 = (f32[64,128]{1,0:T(8,128)S(1)}, f32[64,128]{1,0:T(8,128)}, u32[]{:S(2)}) copy-start(f32[64,128]{1,0:T(8,128)} %spread_ref.1) | copy-start | bytes 98308
  29.1 12.7 %copy-start.6 = (bf16[256,512]{1,0:T(8,128)(2,1)S(1)}, bf16[256,512]{1,0:T(8,128)(2,1)}, u32[]{:S(2)}) copy-start(bf16[256,512]{1,0:T(8,128)(2,1)} %constant.17.clone.flow_ref) | copy-start | bytes 786436
  29.1 12.7 %copy-start.7 = (bf16[256,512]{1,0:T(8,128)(2,1)S(1)}, bf16[256,512]{1,0:T(8,128)(2,1)}, u32[]{:S(2)}) copy-start(bf16[256,512]{1,0:T(8,128)(2,1)} %constant.16.clone.fhigh_ref) | copy-start | bytes 786436

commit v4 on v3

--- a/solution.py
+++ b/solution.py
@@ -14,7 +14,7 @@
 F32 = jnp.float32
 NT = (((1,), (1,)), ((), ()))
 NN = (((1,), (0,)), ((), ()))
-VMEM_BYTES = 62 * 1024 * 1024
+VMEM_BYTES = 67043328
 LANES = 128
 SUBLANES = 8
 
@@ -66,14 +66,27 @@
     return [np.asarray(a, np.float32) for a in (mu, diagonal, packed(up), packed(up * down))]
 
 
-def meet(axis):
-    count = lax.axis_size(axis)
-    me = lax.axis_index(axis)
+def place_of_device(index):
+    sections = lax.axis_size("tm")
+    return {"tm": lax.rem(index, sections), "lev": lax.div(index, sections)}
+
+
+def own_index():
+    return lax.axis_index("lev") * lax.axis_size("tm") + lax.axis_index("tm")
+
+
+def meet():
+    count = lax.axis_size("tm") * lax.axis_size("lev")
+    me = own_index()
     barrier = pltpu.get_barrier_semaphore()
-    for d in range(1, count):
+
+    def greet(d, carry):
         pl.semaphore_signal(
-            barrier, inc=1, device_id={axis: lax.rem(me + d, count)}, device_id_type=pl.DeviceIdType.MESH
+            barrier, inc=1, device_id=place_of_device(lax.rem(me + d, count)), device_id_type=pl.DeviceIdType.MESH
         )
+        return carry
+
+    lax.fori_loop(1, count, greet, 0)
     pl.semaphore_wait(barrier, count - 1)
 
 
@@ -105,21 +118,12 @@
     return tall, (lat_rows // tall) * (lon_cols // LANES)
 
 
-def sort_kernel(
-    lon_cols, tall, bins, mine, cell_ref, innov_ref, damp_ref, tangent_ref, out_ref, rate_ref,
-    lane_from, sub_from, swaps, sent, landed,
+def sort_message(
+    lon_cols, tall, bins, mine, cell_ref, innov_ref, damp_ref, out_ref, lane_from, sub_from, swaps
 ):
-    levels, deep, _ = innov_ref.shape
+    deep = cell_ref.shape[0]
+    levels = innov_ref.shape[0] // deep
     sections = out_ref.shape[0]
-    me = lax.axis_index("tm")
-    meet("tm")
-    copies = rate_copies(sections - 1, tangent_ref, rate_ref, sent, landed)
-
-    @pl.when(me == sections - 1)
-    def _():
-        for copy in copies:
-            copy.start()
-
     blocks = deep // SUBLANES
     low_bits, mid_bits, top_bits = (n.bit_length() - 1 for n in (blocks, SUBLANES, LANES))
     mid_end = low_bits + mid_bits
@@ -214,7 +218,7 @@
                 out_ref[s, k * deep : (k + 1) * deep, :] = jnp.zeros((deep, LANES), F32)
 
     def move(p, carry):
-        values = [innov_ref[p, v * SUBLANES : (v + 1) * SUBLANES, :] for v in range(blocks)]
+        values = [innov_ref[pl.ds(v * SUBLANES * levels + p, SUBLANES, stride=levels), :] for v in range(blocks)]
         for kind, slot in plan:
             if kind == "swap":
                 slot, bit = slot
@@ -235,60 +239,10 @@
 
     lax.fori_loop(0, levels, move, 0)
 
-    @pl.when(me == sections - 1)
-    def _():
-        for copy in copies:
-            copy.wait_send()
-
-    @pl.when(me != sections - 1)
-    def _():
-        copies[0].wait_recv()
-
-
-def sorted_message(cells, innov, damp, tangent, sections, mine, lat_rows, lon_cols):
-    levels, deep, _ = innov.shape
-    blocks = deep // SUBLANES
-    low_bits, mid_bits, top_bits = (n.bit_length() - 1 for n in (blocks, SUBLANES, LANES))
-    all_bits = low_bits + mid_bits + top_bits
-    tall, bins = bin_shape(lat_rows, lon_cols)
-    swap_count = sum(min(stage, low_bits) for stage in range(1, all_bits + 1))
-    return pl.pallas_call(
-        functools.partial(sort_kernel, lon_cols, tall, bins, mine),
-        in_specs=[pl.BlockSpec(memory_space=pltpu.VMEM)] * 3 + [pl.BlockSpec(memory_space=pl.ANY)],
-        out_specs=[pl.BlockSpec(memory_space=pltpu.VMEM), pl.BlockSpec(memory_space=pl.ANY)],
-        out_shape=[
-            jax.ShapeDtypeStruct((sections, (mine + 1) * deep + SUBLANES, LANES), F32),
-            jax.ShapeDtypeStruct((mine * lat_rows, lon_cols), F32),
-        ],
-        scratch_shapes=[
-            pltpu.VMEM((top_bits, blocks, SUBLANES, LANES), jnp.int32),
-            pltpu.VMEM((top_bits + mid_bits, blocks, SUBLANES, LANES), jnp.int32),
-            pltpu.VMEM((swap_count, max(1, blocks // 2), SUBLANES, LANES), jnp.int32),
-            pltpu.SemaphoreType.DMA((sections,)),
-            pltpu.SemaphoreType.DMA,
-        ],
-        compiler_params=pltpu.CompilerParams(
-            collective_id=2, has_side_effects=True, vmem_limit_bytes=10 * 2**20
-        ),
-        cost_estimate=pl.CostEstimate(flops=2**30, bytes_accessed=2**21, transcendentals=0),
-    )(cells, innov, damp, tangent)
-
-
-def forcing_kernel(
-    mine, extra, tall, message_ref, tangent_ref, out_ref, rate_ref, run_ref, edge_ref, edge_sem, sent, landed,
-):
+
+def forcing_fields(mine, extra, tall, message_ref, out_ref, run_ref, edge_ref, edge_sem):
     times = message_ref.shape[0]
     bins = out_ref.shape[1]
-    me = lax.axis_index("tm")
-    meet("tm")
-    traffic = [rate_copies(t, tangent_ref, rate_ref.at[t - 1], sent, landed.at[t]) for t in range(1, times - 1)]
-    for t, copies in enumerate(traffic, 1):
-
-        @pl.when(me == t)
-        def _():
-            for copy in copies:
-                copy.start()
-
     deep = (message_ref.shape[1] - SUBLANES) // (mine + 1)
     chunks = deep // 2
     span = tall * LANES
@@ -347,50 +301,13 @@
         return carry
 
     lax.fori_loop(0, bins, place_bin, 0)
-    for t, copies in enumerate(traffic, 1):
-
-        @pl.when(me == t)
-        def _():
-            for copy in copies:
-                copy.wait_send()
-
-        @pl.when(me != t)
-        def _():
-            copies[0].wait_recv()
-
-
-def forcing_fields(message, tangent, mine, extra, lat_rows, lon_cols):
-    times = message.shape[0]
-    tall, bins = bin_shape(lat_rows, lon_cols)
-    deep = (message.shape[1] - SUBLANES) // (mine + 1)
-    places = -(-(deep // 2 + bins - 1) // 4) * 4 + 1
-    return pl.pallas_call(
-        functools.partial(forcing_kernel, mine, extra, tall),
-        in_specs=[pl.BlockSpec(memory_space=pltpu.VMEM), pl.BlockSpec(memory_space=pl.ANY)],
-        out_specs=[pl.BlockSpec(memory_space=pltpu.VMEM), pl.BlockSpec(memory_space=pl.ANY)],
-        out_shape=[
-            jax.ShapeDtypeStruct((times, bins, mine * tall, LANES), F32),
-            jax.ShapeDtypeStruct((times - 2, mine * lat_rows, lon_cols), F32),
-        ],
-        scratch_shapes=[
-            pltpu.VMEM((times, places, mine * tall, LANES), F32),
-            pltpu.SMEM((times, LANES), F32),
-            pltpu.SemaphoreType.DMA,
-            pltpu.SemaphoreType.DMA((times,)),
-            pltpu.SemaphoreType.DMA((times,)),
-        ],
-        compiler_params=pltpu.CompilerParams(
-            collective_id=3, has_side_effects=True, vmem_limit_bytes=4 * times * places * mine * tall * LANES + 10 * 2**20
-        ),
-        cost_estimate=pl.CostEstimate(flops=2**33, bytes_accessed=2**22, transcendentals=0),
-    )(message, tangent)
 
 
 def lanes_at(value, index):
     return jnp.take_along_axis(value, jnp.broadcast_to(index, value.shape), axis=1, mode="promise_in_bounds")
 
 
-def legendre_tables(half, mu_ref, diag_ref, up_ref, both_ref, high, low, left, right):
+def legendre_tables(between, half, mu_ref, diag_ref, up_ref, both_ref, high, low, left, right):
     groups, width = mu_ref.shape
     waves = high.shape[1]
     pack = width // half
@@ -416,7 +333,9 @@
         return value, one
 
     zero = 0.0 * mu_ref[...]
-    lax.fori_loop(0, waves, advance, (zero, zero), unroll=8)
+    state = lax.fori_loop(0, SUBLANES, advance, (zero, zero), unroll=8)
+    between()
+    lax.fori_loop(SUBLANES, waves, advance, state, unroll=8)
 
     def split(g, carry):
         for i, ref in enumerate((left, right)):
@@ -428,91 +347,154 @@
     lax.fori_loop(0, groups, split, 0, unroll=4)
 
 
-def exchange_kernel(
-    half, message_ref, mu_ref, diag_ref, up_ref, both_ref, out_ref, high_ref, low_ref,
-    high, low, left, right, sent, landed, own, stored,
+def whole_kernel(
+    lon_cols, tall, bins, mine, half,
+    cell_ref, innov_ref, damp_ref, mu_ref, diag_ref, up_ref, both_ref, spread_ref, fhigh_ref, flow_ref, tangent_hbm,
+    arrived_ref,
+    message, received, lane_from, sub_from, swaps, left, right, run_ref, edge_ref,
+    field_ref, tail_ref, high, low, tangent_ref, even, odd, packed, total, adjoint, order, outgoing,
+    edge_sem, rate_sent, rate_landed, sent, landed, own_sem, spread_sent, spread_landed,
 ):
-    sections = lax.axis_size("tm")
+    sections = message.shape[0]
     me = lax.axis_index("tm")
-    meet("tm")
+    extra = mine * damp_ref.shape[1] // LANES
+    deep = cell_ref.shape[0]
+    rows = tangent_ref.shape[1]
+    own_rates = rates_for(tangent_hbm, rows, me)
+
+    @pl.when(me > 0)
+    def _():
+        pltpu.make_async_copy(own_rates, tangent_ref.at[me], rate_landed.at[me]).start()
+
+    meet()
+    traffic = {
+        t: rate_copies(t, tangent_hbm, tangent_ref.at[t], rate_sent, rate_landed.at[t]) for t in range(1, sections)
+    }
+
+    def depart(t):
+        @pl.when(me == t)
+        def _():
+            for copy in traffic[t]:
+                copy.start()
+
+    depart(sections - 1)
+    sort_message(lon_cols, tall, bins, mine, cell_ref, innov_ref, damp_ref, message, lane_from, sub_from, swaps)
     copies = []
     for d in range(1, sections):
         peer = lax.rem(me + d, sections)
         copies.append(
             pltpu.make_async_remote_copy(
-                src_ref=message_ref.at[peer],
-                dst_ref=out_ref.at[me],
+                src_ref=message.at[peer],
+                dst_ref=received.at[me],
                 send_sem=sent.at[d],
                 recv_sem=landed.at[d],
                 device_id={"tm": peer},
                 device_id_type=pl.DeviceIdType.MESH,
             )
         )
-        copies[-1].start()
-    keep = pltpu.make_async_copy(message_ref.at[me], out_ref.at[me], own)
-    keep.start()
-    legendre_tables(half, mu_ref, diag_ref, up_ref, both_ref, high, low, left, right)
-    saves = [
-        pltpu.make_async_copy(high, high_ref, stored.at[0]),
-        pltpu.make_async_copy(low, low_ref, stored.at[1]),
-    ]
-    for save in saves:
-        save.start()
+    keep = pltpu.make_async_copy(message.at[me], received.at[me], own_sem)
+
+    def between():
+        for copy in copies:
+            copy.start()
+        keep.start()
+        for t in range(1, sections - 1):
+            depart(t)
+
+    legendre_tables(between, half, mu_ref, diag_ref, up_ref, both_ref, high, low, left, right)
     keep.wait()
-    for save in saves:
-        save.wait()
     for copy in copies:
         copy.wait()
-
-
-def exchanged(message, lat_rows, waves):
+    base = (mine + 1) * deep
+    for t in range(sections):
+        tail_ref[t] = received[t, base : base + SUBLANES, :]
+    forcing_fields(mine, extra, tall, received, field_ref, run_ref, edge_ref, edge_sem)
+
+    def rates_at(t):
+        pltpu.make_async_copy(own_rates, tangent_ref.at[t], rate_landed.at[t]).wait()
+        return tangent_ref[t]
+
+    sweep_steps(
+        rates_at, field_ref, tail_ref, high, low, spread_ref, fhigh_ref, flow_ref,
+        outgoing, even, odd, packed, total, adjoint, order,
+    )
+    for t, leaving in traffic.items():
+
+        @pl.when(me == t)
+        def _():
+            for copy in leaving:
+                copy.wait_send()
+
+    deal_blocks(outgoing, arrived_ref, spread_sent, spread_landed, own_sem)
+
+
+def adjoint_totals(cells, innov, damp, spread, tangent, sections, blocks, mine, lat_rows, lon_cols):
+    deep = cells.shape[0]
+    waves = damp.shape[1]
+    columns = deep // SUBLANES
+    low_bits, mid_bits, top_bits = (n.bit_length() - 1 for n in (columns, SUBLANES, LANES))
+    all_bits = low_bits + mid_bits + top_bits
+    tall, bins = bin_shape(lat_rows, lon_cols)
+    swap_count = sum(min(stage, low_bits) for stage in range(1, all_bits + 1))
     mu, diagonal, up, both = legendre_coefficients(lat_rows, waves)
     groups, width = mu.shape
-    sections = message.shape[0]
-    table = jax.ShapeDtypeStruct((groups, waves, width), BF16)
-    vmem = pl.BlockSpec(memory_space=pltpu.VMEM)
+    fourier = fourier_rows(lon_cols, waves)
+    fhigh = fourier.astype(jnp.bfloat16)
+    flow = (fourier - fhigh.astype(np.float32)).astype(jnp.bfloat16)
+    message = (sections, (mine + 1) * deep + SUBLANES, LANES)
+    places = -(-(deep // 2 + bins - 1) // 4) * 4 + 1
+    rows = mine * lat_rows
+    group = 4 * mine
+    deal = 2 * waves * (waves // sections) // LANES // blocks
+    count = blocks * sections
+    vmem, anywhere = pl.BlockSpec(memory_space=pltpu.VMEM), pl.BlockSpec(memory_space=pl.ANY)
     return pl.pallas_call(
-        functools.partial(exchange_kernel, lat_rows // 2),
-        in_specs=[vmem] * 5,
-        out_specs=[vmem, pl.BlockSpec(memory_space=pl.ANY), pl.BlockSpec(memory_space=pl.ANY)],
-        out_shape=[jax.ShapeDtypeStruct(message.shape, F32), table, table],
+        functools.partial(whole_kernel, lon_cols, tall, bins, mine, lat_rows // 2),
+        in_specs=[vmem] * 10 + [anywhere],
+        out_specs=vmem,
+        out_shape=jax.ShapeDtypeStruct((count, mine * deal, LANES), F32),
         scratch_shapes=[
+            pltpu.VMEM(message, F32),
+            pltpu.VMEM(message, F32),
+            pltpu.VMEM((top_bits, columns, SUBLANES, LANES), jnp.int32),
+            pltpu.VMEM((top_bits + mid_bits, columns, SUBLANES, LANES), jnp.int32),
+            pltpu.VMEM((swap_count, max(1, columns // 2), SUBLANES, LANES), jnp.int32),
+            pltpu.VMEM((waves * groups, LANES), F32),
+            pltpu.VMEM((waves * groups, LANES), F32),
+            pltpu.VMEM((sections, places, mine * tall, LANES), F32),
+            pltpu.SMEM((sections, LANES), F32),
+            pltpu.VMEM((sections, bins, mine * tall, LANES), F32),
+            pltpu.VMEM((sections, SUBLANES, LANES), F32),
             pltpu.VMEM((groups, waves, width), BF16),
             pltpu.VMEM((groups, waves, width), BF16),
-            pltpu.VMEM((waves * groups, LANES), F32),
-            pltpu.VMEM((waves * groups, LANES), F32),
+            pltpu.VMEM((sections, rows, lon_cols), F32),
+            pltpu.VMEM((waves * group, LANES), F32),
+            pltpu.VMEM((waves * group, LANES), F32),
+            pltpu.VMEM((waves * group, LANES), F32),
+            pltpu.VMEM((waves * group, LANES), F32),
+            pltpu.VMEM((rows, lon_cols), F32),
+            pltpu.VMEM((2 * waves, LANES), F32),
+            pltpu.VMEM((count, mine * deal, LANES), F32),
+            pltpu.SemaphoreType.DMA,
+            pltpu.SemaphoreType.DMA((sections,)),
+            pltpu.SemaphoreType.DMA((sections,)),
             pltpu.SemaphoreType.DMA((sections,)),
             pltpu.SemaphoreType.DMA((sections,)),
             pltpu.SemaphoreType.DMA,
-            pltpu.SemaphoreType.DMA((2,)),
+            pltpu.SemaphoreType.DMA((count,)),
+            pltpu.SemaphoreType.DMA((count,)),
         ],
         compiler_params=pltpu.CompilerParams(
-            collective_id=0, has_side_effects=True, vmem_limit_bytes=16 * 2**20
+            collective_id=0, has_side_effects=True, vmem_limit_bytes=VMEM_BYTES
         ),
-        cost_estimate=pl.CostEstimate(flops=2**32, bytes_accessed=2**23, transcendentals=0),
-    )(message, mu, diagonal, up, both)
-
-
-def gather_kernel(total_ref, out_ref, sent, landed, own):
-    sections, groups = lax.axis_size("tm"), lax.axis_size("lev")
-    count = sections * groups
-    me = lax.axis_index("lev") * sections + lax.axis_index("tm")
-
-    def place(index):
-        return {"tm": lax.rem(index, sections), "lev": lax.div(index, sections)}
-
-    barrier = pltpu.get_barrier_semaphore()
-
-    def greet(d, carry):
-        pl.semaphore_signal(
-            barrier, inc=1, device_id=place(lax.rem(me + d, count)), device_id_type=pl.DeviceIdType.MESH
-        )
-        return carry
-
-    lax.fori_loop(1, count, greet, 0)
-    keep = pltpu.make_async_copy(total_ref.at[me], out_ref.at[me], own)
-    keep.start()
-    pl.semaphore_wait(barrier, count - 1)
+        cost_estimate=pl.CostEstimate(flops=2**34, bytes_accessed=2**24, transcendentals=0),
+    )(cells, innov, damp, mu, diagonal, up, both, spread, fhigh, flow, tangent)
+
+
+def deal_blocks(total_ref, out_ref, sent, landed, own_sem):
+    count = total_ref.shape[0]
+    me = own_index()
+    keep = pltpu.make_async_copy(total_ref.at[me], out_ref.at[me], own_sem)
 
     def copy_to(d):
         peer = lax.rem(me + d, count)
@@ -521,7 +503,7 @@
             dst_ref=out_ref.at[me],
             send_sem=sent.at[d],
             recv_sem=landed.at[d],
-            device_id=place(peer),
+            device_id=place_of_device(peer),
             device_id_type=pl.DeviceIdType.MESH,
         )
 
@@ -534,69 +516,18 @@
         return carry
 
     lax.fori_loop(1, count, send, 0)
+    keep.start()
     keep.wait()
     lax.fori_loop(1, count, finish, 0)
 
 
-def gathered(total):
-    count = total.shape[0]
-    vmem = pl.BlockSpec(memory_space=pltpu.VMEM)
-    return pl.pallas_call(
-        gather_kernel,
-        in_specs=[vmem],
-        out_specs=vmem,
-        out_shape=jax.ShapeDtypeStruct(total.shape, F32),
-        scratch_shapes=[
-            pltpu.SemaphoreType.DMA((count,)),
-            pltpu.SemaphoreType.DMA((count,)),
-            pltpu.SemaphoreType.DMA,
-        ],
-        compiler_params=pltpu.CompilerParams(collective_id=1, has_side_effects=True, vmem_limit_bytes=4 * 2**20),
-        cost_estimate=pl.CostEstimate(flops=2**30, bytes_accessed=2**20, transcendentals=0),
-    )(total)
-
-
-def sweep_kernel(
-    base, field_hbm, own_hbm, rate_hbm, later_hbm, message_hbm, spread_ref, fhigh_ref, flow_ref, high_hbm, low_hbm,
-    out_ref, field_ref, tangent_ref, tail_ref, high, low, even, odd, packed, total, adjoint, order,
-    field_sem, tangent_sem, tail_sem, table_sem,
+def sweep_steps(
+    rates_at, field_ref, tail_ref, high, low, spread_ref, fhigh_ref, flow_ref,
+    out_ref, even, odd, packed, total, adjoint, order,
 ):
-    times, rows, lon_cols = tangent_ref.shape
+    times = field_ref.shape[0]
+    rows, lon_cols = adjoint.shape
     sections = lax.axis_size("tm")
-    load_tail = pltpu.make_async_copy(message_hbm.at[:, pl.ds(base, SUBLANES), :], tail_ref, tail_sem)
-    load_tables = [
-        pltpu.make_async_copy(high_hbm, high, table_sem.at[0]),
-        pltpu.make_async_copy(low_hbm, low, table_sem.at[1]),
-    ]
-
-    def load_field(t):
-        return pltpu.make_async_copy(field_hbm.at[t], field_ref.at[t], field_sem.at[t])
-
-    me = lax.axis_index("tm")
-    own = rates_for(own_hbm, rows, me)
-
-    def load_tangent(t):
-        return pltpu.make_async_copy(own, tangent_ref.at[t], tangent_sem.at[t])
-
-    def start_tangent(t):
-        @pl.when(me == t)
-        def _():
-            load_tangent(t).start()
-
-        @pl.when(me != t)
-        def _():
-            source = rate_hbm if t == times - 1 else later_hbm.at[t - 1]
-            pltpu.make_async_copy(source, tangent_ref.at[t], tangent_sem.at[t]).start()
-
-    load_field(times - 1).start()
-    load_tail.start()
-    for load in load_tables:
-        load.start()
-    start_tangent(times - 1)
-    for t in range(times - 2, -1, -1):
-        load_field(t).start()
-        if t > 0:
-            start_tangent(t)
     bins = field_ref.shape[1]
     groups, waves, width = high.shape
     lat_rows = width * groups * 2 // waves
@@ -621,8 +552,6 @@
         lax.broadcasted_iota(jnp.int32, (waves, LANES), 0) % (LANES // half)
     )
 
-    load_tail.wait()
-
     def damp_of(t):
         index = 2 * (lane % (waves // 2)) + lane // (waves // 2)
         row = lax.broadcasted_iota(jnp.int32, (group, LANES), 0) % mid // 2
@@ -632,7 +561,6 @@
         return lanes_at(value, index)
 
     def analyse(t):
-        load_field(t).wait()
         field = [
             jnp.concatenate([field_ref[t, h + i, k * tall : (k + 1) * tall, :] for i in range(across)], 1)
             for k in range(levels)
@@ -703,11 +631,6 @@
         analyse(t)
         damp = damp_of(t)
 
-        @pl.when(s == 0)
-        def _():
-            for load in load_tables:
-                load.wait()
-
         def wave(g, inner):
             for i, value in enumerate(spectral_of(g)):
                 packed[place_of(g, i), :] = value
@@ -728,8 +651,7 @@
         )
         upper, lower = halves(synth)
         gridded = dot(upper, fhigh_ref[...], NN) + dot(lower, fhigh_ref[...], NN) + dot(upper, flow_ref[...], NN)
-        load_tangent(t).wait()
-        adjoint[...] = tangent_ref[t] * adjoint[...] + gridded
+        adjoint[...] = rates_at(t) * adjoint[...] + gridded
         return carry
 
     lax.fori_loop(0, times - 1, step, 0)
@@ -763,44 +685,6 @@
                 out_ref[b * sections + s, k * rows : (k + 1) * rows, :] = value[b * rows : (b + 1) * rows]
 
 
-def sweep(fields, tangent, rate, later, message, spread, high, low, lat_rows, base, sections, blocks):
-    times = fields.shape[0]
-    rows, lon_cols = rate.shape
-    levels = rows // lat_rows
-    group = 4 * levels
-    groups, waves, width = high.shape
-    fourier = fourier_rows(lon_cols, waves)
-    fhigh = fourier.astype(jnp.bfloat16)
-    flow = (fourier - fhigh.astype(np.float32)).astype(jnp.bfloat16)
-    deal = 2 * waves * (waves // sections) // LANES // blocks
-    vmem, hbm = pl.BlockSpec(memory_space=pltpu.VMEM), pl.BlockSpec(memory_space=pl.ANY)
-    return pl.pallas_call(
-        functools.partial(sweep_kernel, base),
-        in_specs=[hbm, hbm, hbm, hbm, hbm, vmem, vmem, vmem, hbm, hbm],
-        out_specs=vmem,
-        out_shape=jax.ShapeDtypeStruct((blocks * sections, levels * deal, LANES), F32),
-        scratch_shapes=[
-            pltpu.VMEM(fields.shape, F32),
-            pltpu.VMEM((times, rows, lon_cols), F32),
-            pltpu.VMEM((times, SUBLANES, LANES), F32),
-            pltpu.VMEM((groups, waves, width), BF16),
-            pltpu.VMEM((groups, waves, width), BF16),
-            pltpu.VMEM((waves * group, LANES), F32),
-            pltpu.VMEM((waves * group, LANES), F32),
-            pltpu.VMEM((waves * group, LANES), F32),
-            pltpu.VMEM((waves * group, LANES), F32),
-            pltpu.VMEM((rows, lon_cols), F32),
-            pltpu.VMEM((2 * waves, LANES), F32),
-            pltpu.SemaphoreType.DMA((times,)),
-            pltpu.SemaphoreType.DMA((times,)),
-            pltpu.SemaphoreType.DMA,
-            pltpu.SemaphoreType.DMA((2,)),
-        ],
-        compiler_params=pltpu.CompilerParams(vmem_limit_bytes=24 * 2**20),
-        cost_estimate=pl.CostEstimate(flops=2**34, bytes_accessed=2**22, transcendentals=0),
-    )(fields, tangent, rate, later, message, spread, fhigh, flow, high, low)
-
-
 def shards(obs_cell, innovation, tangent, damping, spread, vertical):
     sections = lax.axis_size("tm")
     groups = lax.axis_size("lev")
@@ -810,35 +694,19 @@
     mine += mine % 2
     padded = mine * sections
 
-    def pad_levels(value, axis):
-        widths = [(0, 0)] * value.ndim
-        widths[axis] = (0, padded - value.shape[axis])
-        return jnp.pad(value, widths) if padded > value.shape[axis] else value
-
-    count = obs_cell.shape[1]
-    deep = count // LANES
-    message, rate = sorted_message(
-        obs_cell.reshape(deep, LANES),
-        innovation.reshape(lev_dev, deep, LANES),
-        damping[0],
-        tangent.reshape(lev_dev * lat_rows, lon_cols),
-        sections,
-        mine,
-        lat_rows,
-        lon_cols,
+    deep = obs_cell.shape[1] // LANES
+    rates = tangent.reshape(lev_dev * lat_rows, lon_cols)
+    innov = innovation.reshape(lev_dev, deep, LANES).transpose(1, 0, 2).reshape(deep * lev_dev, LANES)
+    total = adjoint_totals(
+        obs_cell.reshape(deep, LANES), innov, damping[0], spread, rates, sections, groups, mine, lat_rows, lon_cols
     )
-    message, high, low = exchanged(message, lat_rows, waves)
-    base = (mine + 1) * deep
-    rates = tangent.reshape(lev_dev * lat_rows, lon_cols)
-    fields, later = forcing_fields(message, rates, mine, mine * waves // LANES, lat_rows, lon_cols)
-    total = sweep(fields, rates, rate, later, message, spread, high, low, lat_rows, base, sections, groups)
 
     block_m = waves // groups
     block_n = waves // sections
     deal = total.shape[1] // mine
-    arrived = gathered(total).reshape(groups, padded, deal * LANES)[:, :lev_dev].reshape(levels, deal * LANES)
-    result = jnp.einsum("kj,kx->jx", vertical, arrived, precision=PRECISE)
-    return result.reshape(levels, block_m, 2, block_n)
+    arrived = total.reshape(groups, padded, deal * LANES)[:, :lev_dev].reshape(levels, deal * LANES)
+    result = jnp.einsum("kx,kj->xj", arrived, vertical, precision=PRECISE)
+    return result.reshape(block_m, 2, block_n, levels).transpose(3, 0, 1, 2)
 
 
 def solution(mesh):

time: 72.6 us -> 63.4 us (0.87)
  Pallas kernels: 66.2 us -> 59.9 us
  local copies, waits for them, and re-layouts: 5.42 us -> 1.19 us
  matrix products: 0.41 us -> 2.11 us
    pallas_call x5 -> x1, Pallas kernels: 66.2 us -> 59.9 us  [adjoint_totals(): pl.pallas_call(functools.partial(whole_kernel, lon_cols, tall, bins, mine...]
    unnamed x25 -> x0, local copies, waits for them, and re-layouts: 4.38 us -> none
    dot_general x1, matrix products: 0.41 us -> 2.11 us  [shards(): result = jnp.einsum('kx,kj->xj', arrived, vertical, precision=PRECISE)]
    another operation x1, local copies, waits for them, and re-layouts: 0.05 us -> 1 us  [shards(): total.reshape(groups, padded, deal * LANES)[:, :lev_dev]]
    dot_general x1, local copies, waits for them, and re-layouts: 1 us -> 0.19 us  [shards(): result = jnp.einsum('kx,kj->xj', arrived, vertical, precision=PRECISE)]
where the time goes in v4:
time: 63.4 us; the launch traced here: 63.2 us
  Pallas kernels  59.9 us (94%)
  matrix products  2.11 us (3%)
  local copies, waits for them, and re-layouts  1.19 us (2%)
    pallas_call x1, Pallas kernels, adjoint_totals(): pl.pallas_call(functools.partial(whole_kernel, lon_cols, tall, bins, mine...  59.9 us
    dot_general x1, matrix products, shards(): result = jnp.einsum('kx,kj->xj', arrived, vertical, precision=PRECISE)  2.11 us

profile of v4, /device:TPU:0, one launch (start us, length us, event | category | flops | bytes accessed | tf_op | source)
XLA Modules:
  0.0 63.2 jit_solution(17107660611130552878)
XLA Ops:
  0.0 59.9 %shard_map.118 = f32[32,16,128]{2,1,0:T(8,128)} custom-call(s32[128,128]{1,0:T(8,128)} %bitcast.22, f32[1024,128]{1,0:T(8,128)} %bitcast.21, f32[64,128]{1,0:T(8,128)} %bitcast.23, f32[32,256]{1,0:T(8,128)} %constant.12.clone.mu_ref, f32[32,256]{1,0:T(8,128)} %constant.13.clone.diag_ref, f32[128,128]{1,0:T(8,128)} %constant.14.clone.up_ref, ...), custom_call_target="tpu_custom_call" | custom-call | flops 17179869184 | bytes 16777216 | tf_op jit(solution)/shard_map/pallas_call | solution.py:451
  59.9 1.0 %reshape_reshape.3 = f32[64,1024]{1,0:T(8,128)S(1)} reshape(f32[32,16,128]{2,1,0:T(8,128)} %shard_map.118) | data formatting | bytes 524288 | tf_op jit(solution)/shard_map/reshape;reshape | solution.py:707
  60.9 0.2 copy.13
  61.1 2.1 %convolution_bitcast_fusion = f32[64,16,2,32]{0,3,2,1:T(8,128)} fusion(f32[16,2,32,64]{3,2,1,0:T(8,128)S(1)} %bitcast.18, f32[64,64]{1,0:T(8,128)} %param.17), kind=kOutput, calls=%fused_computation | convolution fusion | flops 50331648 | bytes 540672 | tf_op jit(solution)/shard_map/kx,kj->xj/dot_general | solution.py:708

commit v5 on v4

--- a/solution.py
+++ b/solution.py
@@ -119,7 +119,7 @@
 
 
 def sort_message(
-    lon_cols, tall, bins, mine, cell_ref, innov_ref, damp_ref, out_ref, lane_from, sub_from, swaps
+    lon_cols, tall, bins, mine, target, ready, cell_ref, innov_ref, damp_ref, out_ref, lane_from, sub_from, swaps
 ):
     deep = cell_ref.shape[0]
     levels = innov_ref.shape[0] // deep
@@ -213,11 +213,11 @@
         rows = [damp_ref[pl.ds(place + k, 1), :] for k in range(mine)]
         tail = rows + [edges, jnp.zeros((SUBLANES - extra - 1, LANES), F32)]
         out_ref[s, base : base + SUBLANES, :] = jnp.concatenate(tail, 0)
-        for k in range(mine):
-            if s * mine + k >= levels:
-                out_ref[s, k * deep : (k + 1) * deep, :] = jnp.zeros((deep, LANES), F32)
-
-    def move(p, carry):
+
+    def move(i, carry):
+        ready(i - 1)
+        dest, k = target(i)
+        p = jnp.minimum(dest * mine + k, levels - 1)
         values = [innov_ref[pl.ds(v * SUBLANES * levels + p, SUBLANES, stride=levels), :] for v in range(blocks)]
         for kind, slot in plan:
             if kind == "swap":
@@ -234,10 +234,13 @@
                     jnp.take_along_axis(value, ref[slot, v], axis=axis, mode="promise_in_bounds")
                     for v, value in enumerate(values)
                 ]
-        out_ref[p // mine, pl.ds(pl.multiple_of(p % mine * deep, deep), deep), :] = jnp.concatenate(values, 0).T
+        block = jnp.concatenate(values, 0).T
+        if levels < sections * mine:
+            block = block * (dest * mine + k < levels).astype(F32)
+        out_ref[dest, pl.ds(pl.multiple_of(k * deep, deep), deep), :] = block
         return carry
 
-    lax.fori_loop(0, levels, move, 0)
+    lax.fori_loop(0, sections * mine, move, 0)
 
 
 def forcing_fields(mine, extra, tall, message_ref, out_ref, run_ref, edge_ref, edge_sem):
@@ -268,7 +271,7 @@
         return field[: mine * tall] + field[mine * tall :]
 
     total = chunks + bins - 1
-    unroll = 4
+    unroll = 8
     load.wait()
 
     def walk(s, state):
@@ -349,18 +352,26 @@
 
 def whole_kernel(
     lon_cols, tall, bins, mine, half,
-    cell_ref, innov_ref, damp_ref, mu_ref, diag_ref, up_ref, both_ref, spread_ref, fhigh_ref, flow_ref, tangent_hbm,
+    cell_hbm, innov_hbm, damp_hbm, mu_hbm, diag_hbm, up_hbm, both_hbm, spread_hbm, fhigh_hbm, flow_hbm, tangent_hbm,
     arrived_ref,
+    cell_ref, innov_ref, damp_ref, mu_ref, diag_ref, up_ref, both_ref, spread_ref, fhigh_ref, flow_ref,
     message, received, lane_from, sub_from, swaps, left, right, run_ref, edge_ref,
     field_ref, tail_ref, high, low, tangent_ref, even, odd, packed, total, adjoint, order, outgoing,
-    edge_sem, rate_sent, rate_landed, sent, landed, own_sem, spread_sent, spread_landed,
+    load_sem, edge_sem, rate_sent, rate_landed, sent, landed, own_sem, spread_sent, spread_landed,
 ):
+    inputs = [
+        (cell_hbm, cell_ref), (innov_hbm, innov_ref), (damp_hbm, damp_ref), (mu_hbm, mu_ref), (diag_hbm, diag_ref),
+        (up_hbm, up_ref), (both_hbm, both_ref), (spread_hbm, spread_ref), (fhigh_hbm, fhigh_ref), (flow_hbm, flow_ref),
+    ]
     sections = message.shape[0]
     me = lax.axis_index("tm")
     extra = mine * damp_ref.shape[1] // LANES
     deep = cell_ref.shape[0]
     rows = tangent_ref.shape[1]
     own_rates = rates_for(tangent_hbm, rows, me)
+    loads = [pltpu.make_async_copy(far, near, load_sem.at[i]) for i, (far, near) in enumerate(inputs)]
+    for load in loads:
+        load.start()
 
     @pl.when(me > 0)
     def _():
@@ -370,41 +381,71 @@
     traffic = {
         t: rate_copies(t, tangent_hbm, tangent_ref.at[t], rate_sent, rate_landed.at[t]) for t in range(1, sections)
     }
-
-    def depart(t):
+    early = (0, sections - 2)
+
+    def depart(t, which):
         @pl.when(me == t)
         def _():
-            for copy in traffic[t]:
-                copy.start()
-
-    depart(sections - 1)
-    sort_message(lon_cols, tall, bins, mine, cell_ref, innov_ref, damp_ref, message, lane_from, sub_from, swaps)
-    copies = []
-    for d in range(1, sections):
-        peer = lax.rem(me + d, sections)
-        copies.append(
-            pltpu.make_async_remote_copy(
-                src_ref=message.at[peer],
-                dst_ref=received.at[me],
-                send_sem=sent.at[d],
-                recv_sem=landed.at[d],
-                device_id={"tm": peer},
-                device_id_type=pl.DeviceIdType.MESH,
-            )
+            for i in which:
+                traffic[t][i].start()
+
+    depart(sections - 1, early)
+    for load in loads[:3]:
+        load.wait()
+    half_count = sections // 2
+
+    def target(i):
+        j, k = i // mine, i % mine
+        late = j // half_count
+        side = (1 - me // half_count) * (1 - late) + me // half_count * late
+        return side * half_count + (me + late + j % half_count) % half_count, k
+
+    def piece_copy(dest, piece):
+        size = deep if isinstance(piece, jax.Array) or piece < mine else deep + SUBLANES
+        cut = pl.ds(pl.multiple_of(piece * deep, deep), size)
+        offset = lax.rem(dest - me + sections, sections)
+        return pltpu.make_async_remote_copy(
+            src_ref=message.at[dest, cut, :],
+            dst_ref=received.at[me, cut, :],
+            send_sem=sent.at[offset, piece],
+            recv_sem=landed.at[offset, piece],
+            device_id={"tm": dest},
+            device_id_type=pl.DeviceIdType.MESH,
         )
+
+    def ready(i):
+        @pl.when(i == 0)
+        def _():
+            for d in range(1, sections):
+                piece_copy(lax.rem(me + d, sections), mine).start()
+
+        @pl.when(i >= 0)
+        def _():
+            dest, k = target(i)
+
+            @pl.when(dest != me)
+            def _():
+                piece_copy(dest, k).start()
+
+    sort_message(
+        lon_cols, tall, bins, mine, target, ready, cell_ref, innov_ref, damp_ref, message, lane_from, sub_from, swaps
+    )
     keep = pltpu.make_async_copy(message.at[me], received.at[me], own_sem)
+    for load in loads[3:]:
+        load.wait()
 
     def between():
-        for copy in copies:
-            copy.start()
+        ready(jnp.int32(sections * mine - 1))
         keep.start()
+        depart(sections - 1, [i for i in range(sections - 1) if i not in early])
         for t in range(1, sections - 1):
-            depart(t)
+            depart(t, range(sections - 1))
 
     legendre_tables(between, half, mu_ref, diag_ref, up_ref, both_ref, high, low, left, right)
     keep.wait()
-    for copy in copies:
-        copy.wait()
+    for d in range(1, sections):
+        for piece in range(mine + 1):
+            piece_copy(lax.rem(me + d, sections), piece).wait()
     base = (mine + 1) * deep
     for t in range(sections):
         tail_ref[t] = received[t, base : base + SUBLANES, :]
@@ -442,18 +483,20 @@
     fhigh = fourier.astype(jnp.bfloat16)
     flow = (fourier - fhigh.astype(np.float32)).astype(jnp.bfloat16)
     message = (sections, (mine + 1) * deep + SUBLANES, LANES)
-    places = -(-(deep // 2 + bins - 1) // 4) * 4 + 1
+    places = -(-(deep // 2 + bins - 1) // 8) * 8 + 1
     rows = mine * lat_rows
     group = 4 * mine
     deal = 2 * waves * (waves // sections) // LANES // blocks
     count = blocks * sections
+    inputs = [cells, innov, damp, mu, diagonal, up, both, spread, fhigh, flow]
     vmem, anywhere = pl.BlockSpec(memory_space=pltpu.VMEM), pl.BlockSpec(memory_space=pl.ANY)
     return pl.pallas_call(
         functools.partial(whole_kernel, lon_cols, tall, bins, mine, lat_rows // 2),
-        in_specs=[vmem] * 10 + [anywhere],
+        in_specs=[anywhere] * 11,
         out_specs=vmem,
         out_shape=jax.ShapeDtypeStruct((count, mine * deal, LANES), F32),
-        scratch_shapes=[
+        scratch_shapes=[pltpu.VMEM(value.shape, value.dtype) for value in inputs]
+        + [
             pltpu.VMEM(message, F32),
             pltpu.VMEM(message, F32),
             pltpu.VMEM((top_bits, columns, SUBLANES, LANES), jnp.int32),
@@ -475,11 +518,12 @@
             pltpu.VMEM((rows, lon_cols), F32),
             pltpu.VMEM((2 * waves, LANES), F32),
             pltpu.VMEM((count, mine * deal, LANES), F32),
+            pltpu.SemaphoreType.DMA((len(inputs),)),
             pltpu.SemaphoreType.DMA,
             pltpu.SemaphoreType.DMA((sections,)),
             pltpu.SemaphoreType.DMA((sections,)),
-            pltpu.SemaphoreType.DMA((sections,)),
-            pltpu.SemaphoreType.DMA((sections,)),
+            pltpu.SemaphoreType.DMA((sections, mine + 1)),
+            pltpu.SemaphoreType.DMA((sections, mine + 1)),
             pltpu.SemaphoreType.DMA,
             pltpu.SemaphoreType.DMA((count,)),
             pltpu.SemaphoreType.DMA((count,)),
@@ -488,7 +532,7 @@
             collective_id=0, has_side_effects=True, vmem_limit_bytes=VMEM_BYTES
         ),
         cost_estimate=pl.CostEstimate(flops=2**34, bytes_accessed=2**24, transcendentals=0),
-    )(cells, innov, damp, mu, diagonal, up, both, spread, fhigh, flow, tangent)
+    )(*inputs, tangent)
 
 
 def deal_blocks(total_ref, out_ref, sent, landed, own_sem):

time: 63.4 us -> 58.4 us (0.921)
  Pallas kernels: 59.9 us -> 54.5 us
    pallas_call x1, Pallas kernels: 59.9 us -> 54.5 us  [adjoint_totals(): pl.pallas_call(functools.partial(whole_kernel, lon_cols, tall, bins, mine...]
where the time goes in v5:
time: 58.4 us; the launch traced here: 57.8 us
  Pallas kernels  54.5 us (93%)
  matrix products  2.11 us (4%)
  local copies, waits for them, and re-layouts  1.19 us (2%)
    pallas_call x1, Pallas kernels, adjoint_totals(): pl.pallas_call(functools.partial(whole_kernel, lon_cols, tall, bins, mine...  54.5 us
    dot_general x1, matrix products, shards(): result = jnp.einsum('kx,kj->xj', arrived, vertical, precision=PRECISE)  2.11 us

profile of v5, /device:TPU:0, one launch (start us, length us, event | category | flops | bytes accessed | tf_op | source)
XLA Modules:
  0.0 57.8 jit_solution(11268719767771435630)
XLA Ops:
  0.0 54.5 %shard_map.118 = f32[32,16,128]{2,1,0:T(8,128)} custom-call(s32[128,128]{1,0:T(8,128)} %bitcast.22, f32[1024,128]{1,0:T(8,128)} %bitcast.21, f32[64,128]{1,0:T(8,128)} %bitcast.23, f32[32,256]{1,0:T(8,128)} %constant.12.clone.mu_hbm, f32[32,256]{1,0:T(8,128)} %constant.13.clone.diag_hbm, f32[128,128]{1,0:T(8,128)} %constant.14.clone.up_hbm, ...), custom_call_target="tpu_custom_call" | custom-call | flops 17179869184 | bytes 16777216 | tf_op jit(solution)/shard_map/pallas_call | solution.py:493
  54.5 1.0 %reshape_reshape.3 = f32[64,1024]{1,0:T(8,128)S(1)} reshape(f32[32,16,128]{2,1,0:T(8,128)} %shard_map.118) | data formatting | bytes 524288 | tf_op jit(solution)/shard_map/reshape;reshape | solution.py:751
  55.5 0.2 copy.13
  55.7 2.1 %convolution_bitcast_fusion = f32[64,16,2,32]{0,3,2,1:T(8,128)} fusion(f32[16,2,32,64]{3,2,1,0:T(8,128)S(1)} %bitcast.18, f32[64,64]{1,0:T(8,128)} %param.17), kind=kOutput, calls=%fused_computation | convolution fusion | flops 50331648 | bytes 540672 | tf_op jit(solution)/shard_map/kx,kj->xj/dot_general | solution.py:752

commit v6 on v5

--- a/solution.py
+++ b/solution.py
@@ -214,33 +214,39 @@
         tail = rows + [edges, jnp.zeros((SUBLANES - extra - 1, LANES), F32)]
         out_ref[s, base : base + SUBLANES, :] = jnp.concatenate(tail, 0)
 
-    def move(i, carry):
-        ready(i - 1)
-        dest, k = target(i)
-        p = jnp.minimum(dest * mine + k, levels - 1)
-        values = [innov_ref[pl.ds(v * SUBLANES * levels + p, SUBLANES, stride=levels), :] for v in range(blocks)]
+    def move(j, carry):
+        ready(j - 1)
+        dest = target(j)
+        lists = []
+        for k in range(mine):
+            p = jnp.minimum(dest * mine + k, levels - 1)
+            lists.append(
+                [innov_ref[pl.ds(v * SUBLANES * levels + p, SUBLANES, stride=levels), :] for v in range(blocks)]
+            )
         for kind, slot in plan:
             if kind == "swap":
                 slot, bit = slot
                 firsts = [v for v in range(blocks) if not v >> bit & 1]
                 for pair, v in enumerate(firsts):
                     swap = swaps[slot, pair] != 0
-                    first, second = values[v], values[v | 1 << bit]
-                    values[v] = jnp.where(swap, second, first)
-                    values[v | 1 << bit] = jnp.where(swap, first, second)
+                    for values in lists:
+                        first, second = values[v], values[v | 1 << bit]
+                        values[v] = jnp.where(swap, second, first)
+                        values[v | 1 << bit] = jnp.where(swap, first, second)
             else:
                 ref, axis = (lane_from, 1) if kind == "lane" else (sub_from, 0)
-                values = [
-                    jnp.take_along_axis(value, ref[slot, v], axis=axis, mode="promise_in_bounds")
-                    for v, value in enumerate(values)
-                ]
-        block = jnp.concatenate(values, 0).T
-        if levels < sections * mine:
-            block = block * (dest * mine + k < levels).astype(F32)
-        out_ref[dest, pl.ds(pl.multiple_of(k * deep, deep), deep), :] = block
+                for v in range(blocks):
+                    index = ref[slot, v]
+                    for values in lists:
+                        values[v] = jnp.take_along_axis(values[v], index, axis=axis, mode="promise_in_bounds")
+        for k, values in enumerate(lists):
+            block = jnp.concatenate(values, 0).T
+            if levels < sections * mine:
+                block = block * (dest * mine + k < levels).astype(F32)
+            out_ref[dest, k * deep : (k + 1) * deep, :] = block
         return carry
 
-    lax.fori_loop(0, sections * mine, move, 0)
+    lax.fori_loop(0, sections, move, 0)
 
 
 def forcing_fields(mine, extra, tall, message_ref, out_ref, run_ref, edge_ref, edge_sem):
@@ -352,16 +358,17 @@
 
 def whole_kernel(
     lon_cols, tall, bins, mine, half,
-    cell_hbm, innov_hbm, damp_hbm, mu_hbm, diag_hbm, up_hbm, both_hbm, spread_hbm, fhigh_hbm, flow_hbm, tangent_hbm,
-    arrived_ref,
-    cell_ref, innov_ref, damp_ref, mu_ref, diag_ref, up_ref, both_ref, spread_ref, fhigh_ref, flow_ref,
+    cell_hbm, innov_hbm, damp_hbm, mu_hbm, diag_hbm, up_hbm, both_hbm, spread_hbm, fhigh_hbm, flow_hbm, vertical_hbm, tangent_hbm,
+    result_ref,
+    cell_ref, innov_ref, damp_ref, mu_ref, diag_ref, up_ref, both_ref, spread_ref, fhigh_ref, flow_ref, vertical_ref,
     message, received, lane_from, sub_from, swaps, left, right, run_ref, edge_ref,
-    field_ref, tail_ref, high, low, tangent_ref, even, odd, packed, total, adjoint, order, outgoing,
+    field_ref, tail_ref, high, low, tangent_ref, even, odd, packed, total, adjoint, order, outgoing, arrived_ref, flat,
     load_sem, edge_sem, rate_sent, rate_landed, sent, landed, own_sem, spread_sent, spread_landed,
 ):
     inputs = [
         (cell_hbm, cell_ref), (innov_hbm, innov_ref), (damp_hbm, damp_ref), (mu_hbm, mu_ref), (diag_hbm, diag_ref),
         (up_hbm, up_ref), (both_hbm, both_ref), (spread_hbm, spread_ref), (fhigh_hbm, fhigh_ref), (flow_hbm, flow_ref),
+        (vertical_hbm, vertical_ref),
     ]
     sections = message.shape[0]
     me = lax.axis_index("tm")
@@ -394,15 +401,13 @@
         load.wait()
     half_count = sections // 2
 
-    def target(i):
-        j, k = i // mine, i % mine
+    def target(j):
         late = j // half_count
         side = (1 - me // half_count) * (1 - late) + me // half_count * late
-        return side * half_count + (me + late + j % half_count) % half_count, k
+        return side * half_count + (me + late + j % half_count) % half_count
 
     def piece_copy(dest, piece):
-        size = deep if isinstance(piece, jax.Array) or piece < mine else deep + SUBLANES
-        cut = pl.ds(pl.multiple_of(piece * deep, deep), size)
+        cut = pl.ds(piece * mine * deep, deep + SUBLANES if piece else mine * deep)
         offset = lax.rem(dest - me + sections, sections)
         return pltpu.make_async_remote_copy(
             src_ref=message.at[dest, cut, :],
@@ -413,19 +418,19 @@
             device_id_type=pl.DeviceIdType.MESH,
         )
 
-    def ready(i):
-        @pl.when(i == 0)
+    def ready(j):
+        @pl.when(j == 0)
         def _():
             for d in range(1, sections):
-                piece_copy(lax.rem(me + d, sections), mine).start()
-
-        @pl.when(i >= 0)
+                piece_copy(lax.rem(me + d, sections), 1).start()
+
+        @pl.when(j >= 0)
         def _():
-            dest, k = target(i)
+            dest = target(j)
 
             @pl.when(dest != me)
             def _():
-                piece_copy(dest, k).start()
+                piece_copy(dest, 0).start()
 
     sort_message(
         lon_cols, tall, bins, mine, target, ready, cell_ref, innov_ref, damp_ref, message, lane_from, sub_from, swaps
@@ -435,7 +440,7 @@
         load.wait()
 
     def between():
-        ready(jnp.int32(sections * mine - 1))
+        ready(jnp.int32(sections - 1))
         keep.start()
         depart(sections - 1, [i for i in range(sections - 1) if i not in early])
         for t in range(1, sections - 1):
@@ -444,7 +449,7 @@
     legendre_tables(between, half, mu_ref, diag_ref, up_ref, both_ref, high, low, left, right)
     keep.wait()
     for d in range(1, sections):
-        for piece in range(mine + 1):
+        for piece in range(2):
             piece_copy(lax.rem(me + d, sections), piece).wait()
     base = (mine + 1) * deep
     for t in range(sections):
@@ -467,9 +472,19 @@
                 copy.wait_send()
 
     deal_blocks(outgoing, arrived_ref, spread_sent, spread_landed, own_sem)
-
-
-def adjoint_totals(cells, innov, damp, spread, tangent, sections, blocks, mine, lat_rows, lon_cols):
+    count, each, _ = arrived_ref.shape
+    for i in range(count):
+        flat[i * each : (i + 1) * each, :] = arrived_ref[i]
+    upper, lower = halves(vertical_ref[...])
+    deal = each // mine
+    for r in range(deal):
+        high_part, low_part = halves(flat[pl.ds(r, count * mine, stride=deal), :].T)
+        result_ref[r * LANES : (r + 1) * LANES, :] = (
+            dot(high_part, upper, NN) + dot(low_part, upper, NN) + dot(high_part, lower, NN)
+        )
+
+
+def gradient_block(cells, innov, damp, spread, vertical, tangent, sections, blocks, mine, lat_rows, lon_cols):
     deep = cells.shape[0]
     waves = damp.shape[1]
     columns = deep // SUBLANES
@@ -488,13 +503,13 @@
     group = 4 * mine
     deal = 2 * waves * (waves // sections) // LANES // blocks
     count = blocks * sections
-    inputs = [cells, innov, damp, mu, diagonal, up, both, spread, fhigh, flow]
+    inputs = [cells, innov, damp, mu, diagonal, up, both, spread, fhigh, flow, vertical]
     vmem, anywhere = pl.BlockSpec(memory_space=pltpu.VMEM), pl.BlockSpec(memory_space=pl.ANY)
     return pl.pallas_call(
         functools.partial(whole_kernel, lon_cols, tall, bins, mine, lat_rows // 2),
-        in_specs=[anywhere] * 11,
+        in_specs=[anywhere] * (len(inputs) + 1),
         out_specs=vmem,
-        out_shape=jax.ShapeDtypeStruct((count, mine * deal, LANES), F32),
+        out_shape=jax.ShapeDtypeStruct((deal * LANES, vertical.shape[1]), F32),
         scratch_shapes=[pltpu.VMEM(value.shape, value.dtype) for value in inputs]
         + [
             pltpu.VMEM(message, F32),
@@ -518,12 +533,14 @@
             pltpu.VMEM((rows, lon_cols), F32),
             pltpu.VMEM((2 * waves, LANES), F32),
             pltpu.VMEM((count, mine * deal, LANES), F32),
+            pltpu.VMEM((count, mine * deal, LANES), F32),
+            pltpu.VMEM((count * mine * deal, LANES), F32),
             pltpu.SemaphoreType.DMA((len(inputs),)),
             pltpu.SemaphoreType.DMA,
             pltpu.SemaphoreType.DMA((sections,)),
             pltpu.SemaphoreType.DMA((sections,)),
-            pltpu.SemaphoreType.DMA((sections, mine + 1)),
-            pltpu.SemaphoreType.DMA((sections, mine + 1)),
+            pltpu.SemaphoreType.DMA((sections, 2)),
+            pltpu.SemaphoreType.DMA((sections, 2)),
             pltpu.SemaphoreType.DMA,
             pltpu.SemaphoreType.DMA((count,)),
             pltpu.SemaphoreType.DMA((count,)),
@@ -741,15 +758,16 @@
     deep = obs_cell.shape[1] // LANES
     rates = tangent.reshape(lev_dev * lat_rows, lon_cols)
     innov = innovation.reshape(lev_dev, deep, LANES).transpose(1, 0, 2).reshape(deep * lev_dev, LANES)
-    total = adjoint_totals(
-        obs_cell.reshape(deep, LANES), innov, damping[0], spread, rates, sections, groups, mine, lat_rows, lon_cols
+    mixing = vertical
+    if padded > lev_dev:
+        mixing = vertical.reshape(groups, lev_dev, levels)
+        mixing = jnp.pad(mixing, ((0, 0), (0, padded - lev_dev), (0, 0))).reshape(groups * padded, levels)
+    result = gradient_block(
+        obs_cell.reshape(deep, LANES), innov, damping[0], spread, mixing, rates, sections, groups, mine, lat_rows, lon_cols
     )
 
     block_m = waves // groups
     block_n = waves // sections
-    deal = total.shape[1] // mine
-    arrived = total.reshape(groups, padded, deal * LANES)[:, :lev_dev].reshape(levels, deal * LANES)
-    result = jnp.einsum("kx,kj->xj", arrived, vertical, precision=PRECISE)
     return result.reshape(block_m, 2, block_n, levels).transpose(3, 0, 1, 2)
 
 

time: 58.4 us -> 55.2 us (0.945)
  matrix products: 2.11 us -> 0 us
  Pallas kernels: 54.5 us -> 52.8 us
  local copies, waits for them, and re-layouts: 1.19 us -> 1.88 us
    dot_general x1 -> x0, matrix products: 2.11 us -> none  [shards(): result = jnp.einsum('kx,kj->xj', arrived, vertical, precision=PRECISE)]
    unnamed x0 -> x1, local copies, waits for them, and re-layouts: none -> 1.88 us
    pallas_call x1, Pallas kernels: 54.5 us -> 52.8 us  [gradient_block(): pl.pallas_call(functools.partial(whole_kernel, lon_cols, tall, bins, mine...]
    another operation x1 -> x0, local copies, waits for them, and re-layouts: 1 us -> none  [shards(): total.reshape(groups, padded, deal * LANES)[:, :lev_dev]]
where the time goes in v6:
time: 55.2 us; the launch traced here: 54.7 us
  Pallas kernels  52.8 us (96%)
  local copies, waits for them, and re-layouts  1.88 us (3%)
    pallas_call x1, Pallas kernels, gradient_block(): pl.pallas_call(functools.partial(whole_kernel, lon_cols, tall, bins, mine...  52.8 us
    unnamed x1, local copies, waits for them, and re-layouts  1.88 us

profile of v6, /device:TPU:0, one launch (start us, length us, event | category | flops | bytes accessed | tf_op | source)
XLA Modules:
  0.0 54.7 jit_solution(2651422000219272903)
XLA Ops:
  0.0 52.8 %shard_map.118 = f32[1024,64]{1,0:T(8,128)} custom-call(s32[128,128]{1,0:T(8,128)} %bitcast.14, f32[1024,128]{1,0:T(8,128)} %bitcast.13, f32[64,128]{1,0:T(8,128)} %bitcast.15, f32[32,256]{1,0:T(8,128)} %constant.12.clone.mu_hbm, f32[32,256]{1,0:T(8,128)} %constant.13.clone.diag_hbm, f32[128,128]{1,0:T(8,128)} %constant.14.clone.up_hbm, ...), custom_call_target="tpu_custom_call" | custom-call | flops 17179869184 | bytes 16777216 | tf_op jit(solution)/shard_map/pallas_call | solution.py:508
  52.8 1.9 %copy.14 = f32[64,16,2,32]{0,3,2,1:T(8,128)} copy(f32[64,16,2,32]{0,3,2,1:T(8,128)} %bitcast.11) | data formatting | bytes 524288
